TPU v7x, 32 devices: a 4x2x2 block of a 4x4x8 slice. The times are simulated.
32 devices in a mesh: dp: 4 (over y, z), tp: 8 (over x, core).
Axes of the slice: x: 4, y: 2, z: 2, core: 2. Of those that a mesh axis runs over, the one named last changes fastest.
The devices are a block of a 4x4x8 slice.
Arguments:
- layer_in: bfloat16 [8, 1024, 1024], P('dp', 'tp'), parts along dimension 0
- grad_out: bfloat16 [8, 1024, 1024], P('dp', 'tp'), parts along dimension 0
- w_qkv: bfloat16 [1024, 16, 3, 64], P(None, 'tp')
- w_out: bfloat16 [16, 1, 64, 1024], P('tp')
- w_up: bfloat16 [1024, 4096], P(None, 'tp')
- w_down: bfloat16 [4096, 1024], P('tp')
- ln_params: float32 [4, 1024], replicated
Outputs:
- output 1: bfloat16 [8, 1024, 1024], P('dp', 'tp'), parts along dimension 0
- output 2: bfloat16 [4096, 16, 3, 64], P('dp', 'tp'), parts along dimension 0
- output 3: bfloat16 [64, 1, 64, 1024], P(('dp', 'tp')), parts along dimension 0
- output 4: bfloat16 [4096, 4096], P('dp', 'tp'), parts along dimension 0
- output 5: bfloat16 [16384, 1024], P(('dp', 'tp')), parts along dimension 0
- output 6: float32 [16, 1024], P('dp'), parts along dimension 0
There are 4 independent parts. A program takes and returns all parts, laid end to end along the dimension named above; an argument that names none is the same for every part.
All inputs are finite; a program needn't handle non-finite values.
Results may differ from a plain program's by a relative error of at most 0.0061746.
Values are sent between devices in bfloat16 or wider.
A program may use at most 768 MiB of HBM per device.

v0:
```python
import functools

import jax
import jax.numpy as jnp
from jax import lax
from jax.experimental import pallas as pl
from jax.experimental.pallas import tpu as pltpu
from jax.sharding import PartitionSpec as P

NORM_EPS = 1e-5
ROPE_BASE = 10000.0
NEG_BIG = -1e30
LOG2E = 1.4426950408889634
SQRT_HALF = 0.7071067811865476
INV_SQRT_2PI = 0.3989422804014327
F32 = jnp.float32
BF16 = jnp.bfloat16
MESH_ID = pl.DeviceIdType.MESH
BLK = 256
LN_ROWS = 32
GATHER_ORDER = (0, 1, 3, 2)
SCATTER_ORDER = (2, 1, 3, 0)


def pick(index, values):
    out = values[-1]
    for i in range(len(values) - 2, -1, -1):
        out = jnp.where(index == i, values[i], out)
    return out


def dot_nn(lhs, rhs):
    return lax.dot_general(lhs, rhs, (((1,), (0,)), ((), ())), preferred_element_type=F32)


def dot_nt(lhs, rhs):
    return lax.dot_general(lhs, rhs, (((1,), (1,)), ((), ())), preferred_element_type=F32)


def dot_tn(lhs, rhs):
    return lax.dot_general(lhs, rhs, (((0,), (0,)), ((), ())), preferred_element_type=F32)


def fold8(value):
    rows, cols = value.shape
    return jnp.sum(value.reshape(rows // 8, 8, cols), axis=0)


def layer_kernel(nt, x_in, dy_in, wq_in, wo_in, wu_in, wd_in, ln_ref, cos_in, sin_in,
                 gi_out, gq_out, go_out, gu_out, gd_out, gl_out,
                 x_ref, dy_ref, a_ref, m_ref, wq_ref, wo_ref, wu_ref, wd_ref, cos_ref, sin_ref,
                 q_ref, k_ref, v_ref, dc_ref, kt_ref, vt_ref, u_ref, dh_ref, t_ref, p_ref,
                 hp_ref, hm_ref, fp_ref, fm_ref, mu_ref, rstd_ref, s_ref, dp_ref, pt_ref, ds_ref,
                 qm_ref, dcm_ref, dka_ref, dva_ref, dqt_ref, dqkv_ref, ct_ref, acc_ref, gl_ref, gls_ref,
                 gi_ref, gq_ref, go_ref, gu_ref, gd_ref,
                 load_sem, store_sem, ag_send, ag_recv, rs_send, rs_recv, gl_send, gl_recv):
    nc = nt // 2
    batch, seq, width = x_ref.shape
    ff = wu_ref.shape[1]
    rows = x_in.shape[1]
    half = rows // 2
    pair = 2 * rows
    hd = wo_in.shape[0] // 2
    hh = hd // 2
    scale = hd ** -0.5

    me = lax.axis_index("tp")
    chip = me // 2
    core = lax.rem(me, 2)
    partner = chip * 2 + (1 - core)

    def dev(off, which):
        return lax.rem(chip + off, nc) * 2 + which

    plus = dev(1, core)
    minus = dev(nc - 1, core)

    def row0(device):
        return pl.multiple_of(device * rows, rows)

    loads = []

    def load(src, dst):
        loads.append(pltpu.make_async_copy(src, dst, load_sem.at[len(loads)]))
        loads[-1].start()

    barrier = pltpu.get_barrier_semaphore()
    for j in range(1, nt):
        pl.semaphore_signal(barrier, inc=1, device_id={"tp": lax.rem(me + j, nt)}, device_id_type=MESH_ID)

    load(x_in, x_ref.at[:, pl.ds(row0(me), rows), :])
    load(dy_in, dy_ref.at[:, pl.ds(row0(me), rows), :])
    for t, base in ((0, 0), (1, 2 * hd)):
        for part in range(2):
            for g in range(2):
                load(wq_in.at[pl.ds(g * 3 * hd + t * hd + part * hh, hh), :],
                     wq_ref.at[pl.ds(base + part * hd + g * hh, hh), :])
    for g in range(2):
        load(wq_in.at[pl.ds(g * 3 * hd + 2 * hd, hd), :], wq_ref.at[pl.ds(4 * hd + g * hd, hd), :])
    load(cos_in, cos_ref)
    load(sin_in, sin_ref)
    load(wo_in, wo_ref)
    load(wu_in, wu_ref)
    load(wd_in, wd_ref)

    pl.semaphore_wait(barrier, nt - 1)

    def ag(kind, src, dst, b, target):
        return pltpu.make_async_remote_copy(
            src_ref=src, dst_ref=dst, send_sem=ag_send.at[b, kind], recv_sem=ag_recv.at[b, kind],
            device_id={"tp": target}, device_id_type=MESH_ID)

    def rows_of(ref, b, device):
        return ref.at[b, pl.ds(row0(device), rows), :]

    def own(kind, b):
        ref, src = ((x_ref, x_in), (dy_ref, dy_in))[kind % 2]
        target = (plus, minus, partner)[kind // 2]
        return ag(kind, src.at[b], rows_of(ref, b, me), b, target)

    def forward(kind, b):
        if kind == 6:
            return ag(kind, rows_of(x_ref, b, minus), rows_of(x_ref, b, minus), b, plus)
        if kind == 7:
            return ag(kind, rows_of(dy_ref, b, plus), rows_of(dy_ref, b, plus), b, minus)
        ref = (x_ref, dy_ref)[kind % 2]
        source = dev((nc - 1, 1, 2)[(kind - 8) // 2], core)
        return ag(kind, rows_of(ref, b, source), rows_of(ref, b, source), b, partner)

    def arrived(kind, b):
        ref = (x_ref, dy_ref)[kind % 2]
        if kind < 6:
            source = (minus, plus, partner)[kind // 2]
        elif kind < 8:
            source = dev(2, core)
        else:
            source = dev((nc - 1, 1, 2)[(kind - 8) // 2], 1 - core)
        ag(kind, rows_of(ref, b, source), rows_of(ref, b, source), b, partner).wait_recv()

    def send_own(b):
        for kind in (0, 2, 4, 1, 3, 5):
            own(kind, b).start()

    def service_x(b):
        arrived(0, b)
        forward(6, b).start()
        forward(8, b).start()
        arrived(2, b)
        forward(10, b).start()

    def service_dy(b):
        arrived(3, b)
        forward(7, b).start()
        forward(11, b).start()
        arrived(1, b)
        forward(9, b).start()

    def service_far(b):
        arrived(6, b)
        forward(12, b).start()
        arrived(7, b)
        forward(13, b).start()
        arrived(12, b)
        arrived(13, b)

    def rs(kind, src, dst, b, target):
        return pltpu.make_async_remote_copy(
            src_ref=src, dst_ref=dst, send_sem=rs_send.at[b, kind], recv_sem=rs_recv.at[b, kind],
            device_id={"tp": target}, device_id_type=MESH_ID)

    def part_rows(b, device, part):
        if part is None:
            return t_ref.at[b, pl.ds(row0(device), rows), :]
        return t_ref.at[b, pl.ds(pl.multiple_of(device * rows + part * half, half), half), :]

    def to_partner(b, j, off):
        return rs(j, part_rows(b, dev(off, 1 - core), None), p_ref.at[b, j], b, partner)

    def ring(kind, b):
        lo, hi = pl.ds(0, half), pl.ds(half, half)
        if kind == 4:
            return rs(kind, part_rows(b, dev(2, core), 0), hp_ref.at[b], b, plus)
        if kind == 5:
            return rs(kind, part_rows(b, dev(2, core), 1), hm_ref.at[b], b, minus)
        if kind == 6:
            return rs(kind, part_rows(b, plus, 1), fp_ref.at[b, hi, :], b, plus)
        if kind == 7:
            return rs(kind, part_rows(b, plus, 0), fp_ref.at[b, lo, :], b, plus)
        if kind == 8:
            return rs(kind, part_rows(b, minus, 0), fm_ref.at[b, lo, :], b, minus)
        return rs(kind, part_rows(b, minus, 1), fm_ref.at[b, hi, :], b, minus)

    def add_partner(b, j):
        off = pick(j, SCATTER_ORDER)
        target = dev(off, core)
        rs(j, part_rows(b, target, None), p_ref.at[b, j], b, partner).wait_recv()

        @pl.loop(0, rows, step=LN_ROWS)
        def _(i):
            at = pl.ds(pl.multiple_of(target * rows + i, LN_ROWS), LN_ROWS)
            t_ref[b, at, :] += p_ref[b, j, pl.ds(pl.multiple_of(i, LN_ROWS), LN_ROWS), :]

    def ring_after_partner(b, j):
        @pl.when(j == 0)
        def _():
            ring(4, b).start()
            ring(5, b).start()

        @pl.when(j == 1)
        def _():
            ring(6, b).start()

        @pl.when(j == 2)
        def _():
            ring(8, b).start()

    def add_half(b, device, part, ref):
        @pl.loop(0, half, step=LN_ROWS)
        def _(i):
            at = pl.ds(pl.multiple_of(device * rows + part * half + i, LN_ROWS), LN_ROWS)
            t_ref[b, at, :] += ref[b, pl.ds(pl.multiple_of(i, LN_ROWS), LN_ROWS), :]

    def ring_second(b):
        ring(4, b).wait_recv()
        add_half(b, plus, 0, hp_ref)
        ring(7, b).start()
        ring(5, b).wait_recv()
        add_half(b, minus, 1, hm_ref)
        ring(9, b).start()

    def unit(b, cc):
        r0 = pl.multiple_of(cc * pair, pair)
        at = pl.ds(r0, pair)

        @pl.loop(0, pair, step=LN_ROWS)
        def _(i):
            sub = pl.ds(pl.multiple_of(r0 + i, LN_ROWS), LN_ROWS)
            xs = x_ref[b, sub, :].astype(F32)
            mu = jnp.mean(xs, axis=-1, keepdims=True)
            xc = xs - mu
            rstd = lax.rsqrt(jnp.mean(xc * xc, axis=-1, keepdims=True) + NORM_EPS)
            xh = xc * rstd
            mu_ref[b, sub, :] = mu
            rstd_ref[b, sub, :] = rstd
            a_ref[b, sub, :] = (xh * ln_ref[0:1, :] + ln_ref[1:2, :]).astype(BF16)
            m_ref[b, sub, :] = (xh * ln_ref[2:3, :] + ln_ref[3:4, :]).astype(BF16)

        a = a_ref[b, at, :]
        dy = dy_ref[b, at, :]
        cos = cos_ref[at, :]
        sin = sin_ref[at, :]
        q = dot_nt(a, wq_ref[0:2 * hd, :]).astype(BF16).astype(F32)
        q_ref[b, at, :] = (q * cos + pltpu.roll(q, hd, 1) * sin).astype(BF16)
        k = dot_nt(a, wq_ref[2 * hd:4 * hd, :]).astype(BF16).astype(F32)
        k2 = k * cos + pltpu.roll(k, hd, 1) * sin
        k_ref[b, at, :] = k2.astype(BF16)
        kt_ref[b, :, at] = k2.T.astype(BF16)
        v = dot_nt(a, wq_ref[4 * hd:6 * hd, :])
        v_ref[b, at, :] = v.astype(BF16)
        vt_ref[b, :, at] = v.T.astype(BF16)
        dc_ref[b, at, :] = dot_nt(dy, wo_ref[...]).astype(BF16)
        m = m_ref[b, at, :]
        for f in range(0, ff, BLK):
            h = dot_nn(m, wu_ref[:, f:f + BLK])
            du = dot_nt(dy, wd_ref[f:f + BLK, :])
            cdf = 0.5 * (1.0 + lax.erf(h * SQRT_HALF))
            pdf = jnp.exp2(h * h * (-0.5 * LOG2E)) * INV_SQRT_2PI
            u_ref[b, at, f:f + BLK] = (h * cdf).astype(BF16)
            dh_ref[b, at, f:f + BLK] = (du * (cdf + h * pdf)).astype(BF16)
        dh = dh_ref[b, at, :]
        mu = mu_ref[b, at, :]
        rstd = rstd_ref[b, at, :]
        for d in range(0, width, BLK):
            cols = slice(d, d + BLK)
            dm = dot_nt(dh, wu_ref[cols, :])
            xh = (x_ref[b, at, cols].astype(F32) - mu) * rstd
            t_ref[b, at, cols] = dm * ln_ref[2:3, cols]
            acc_ref[2, :, cols] += fold8(dm * xh)
            acc_ref[3, :, cols] += fold8(dm)

    def attention_head(b, h):
        lane = lax.broadcasted_iota(jnp.int32, (1, 2 * hd), 1)
        q_mask = lax.rem(lane // hh, 2) == h
        v_mask = (lane // hd) == h
        qm_ref[...] = jnp.where(q_mask, q_ref[b], jnp.zeros((), BF16))
        dcm_ref[...] = jnp.where(v_mask, dc_ref[b], jnp.zeros((), BF16))
        v_rows = pl.ds(pl.multiple_of(h * hd, hd), hd)
        k_lo = pl.ds(pl.multiple_of(h * hh, hh), hh)
        k_hi = pl.ds(pl.multiple_of(hd + h * hh, hh), hh)
        for qb in range(seq // BLK):
            qs = slice(qb * BLK, (qb + 1) * BLK)
            kl = (qb + 1) * BLK
            qm = qm_ref[qs, :]
            dcm = dcm_ref[qs, :]
            top = None
            for kb in range(qb + 1):
                ks = slice(kb * BLK, (kb + 1) * BLK)
                s = dot_nt(k_ref[b, ks, :], qm)
                if kb == qb:
                    key = lax.broadcasted_iota(jnp.int32, (BLK, BLK), 0)
                    query = lax.broadcasted_iota(jnp.int32, (BLK, BLK), 1)
                    s = jnp.where(key <= query, s, NEG_BIG)
                s_ref[ks, :] = s
                best = jnp.max(s.reshape(BLK // 8, 8, BLK), axis=0)
                top = best if top is None else jnp.maximum(top, best)
            top = jnp.max(top, axis=0, keepdims=True)
            total = jnp.zeros((8, BLK), F32)
            weighted = jnp.zeros((8, BLK), F32)
            for kb in range(qb + 1):
                ks = slice(kb * BLK, (kb + 1) * BLK)
                e = jnp.exp2((s_ref[ks, :] - top) * (scale * LOG2E))
                dpr = dot_nt(v_ref[b, ks, :], dcm)
                s_ref[ks, :] = e
                dp_ref[ks, :] = dpr
                total += fold8(e)
                weighted += fold8(e * dpr)
            inv = 1.0 / jnp.sum(total, axis=0, keepdims=True)
            mean_dp = jnp.sum(weighted, axis=0, keepdims=True) * inv
            for kb in range(qb + 1):
                ks = slice(kb * BLK, (kb + 1) * BLK)
                p = s_ref[ks, :] * inv
                pt_ref[ks, qs] = p.astype(BF16)
                ds_ref[ks, qs] = (p * (dp_ref[ks, :] - mean_dp) * scale).astype(BF16)
            c = dot_nn(vt_ref[b, v_rows, 0:kl], pt_ref[0:kl, qs])
            ct_ref[b, v_rows, qs] = c.astype(BF16)
            kt = jnp.concatenate([kt_ref[b, k_lo, 0:kl], kt_ref[b, k_hi, 0:kl]], axis=0)
            dq = dot_nn(kt, ds_ref[0:kl, qs])
            dqt_ref[k_lo, qs] = dq[0:hh]
            dqt_ref[k_hi, qs] = dq[hh:hd]
        for kb in range(seq // BLK):
            ks = slice(kb * BLK, (kb + 1) * BLK)
            dva_ref[ks, :] += dot_nn(pt_ref[ks, kb * BLK:], dcm_ref[kb * BLK:, :])
            dka_ref[ks, :] += dot_nn(ds_ref[ks, kb * BLK:], qm_ref[kb * BLK:, :])

    def attention_finish(b):
        @pl.loop(0, seq, step=BLK)
        def _(i):
            at = pl.ds(pl.multiple_of(i, BLK), BLK)
            cos = cos_ref[at, :]
            sin = sin_ref[at, :]
            dq = dqt_ref[:, at].T
            dqkv_ref[b, at, 0:2 * hd] = (dq * cos - pltpu.roll(dq, hd, 1) * sin).astype(BF16)
            dk = dka_ref[at, :]
            dqkv_ref[b, at, 2 * hd:4 * hd] = (dk * cos - pltpu.roll(dk, hd, 1) * sin).astype(BF16)
            dqkv_ref[b, at, 4 * hd:6 * hd] = dva_ref[at, :].astype(BF16)

    def input_grad(b, cc):
        at = pl.ds(pl.multiple_of(cc * pair, pair), pair)
        dqkv = dqkv_ref[b, at, :]
        mu = mu_ref[b, at, :]
        rstd = rstd_ref[b, at, :]
        for d in range(0, width, BLK):
            cols = slice(d, d + BLK)
            da = dot_nn(dqkv, wq_ref[:, cols])
            xh = (x_ref[b, at, cols].astype(F32) - mu) * rstd
            t_ref[b, at, cols] += da * ln_ref[0:1, cols]
            acc_ref[0, :, cols] += fold8(da * xh)
            acc_ref[1, :, cols] += fold8(da)

    def finish(b):
        for kind, ref in ((6, fp_ref), (7, fp_ref), (8, fm_ref), (9, fm_ref)):
            ring(kind, b).wait_recv()

        @pl.loop(0, rows, step=LN_ROWS)
        def _(i):
            at = pl.ds(pl.multiple_of(me * rows + i, LN_ROWS), LN_ROWS)
            sub = pl.ds(pl.multiple_of(i, LN_ROWS), LN_ROWS)
            t = t_ref[b, at, :] + fp_ref[b, sub, :] + fm_ref[b, sub, :]
            rstd = rstd_ref[b, at, :]
            xh = (x_ref[b, at, :].astype(F32) - mu_ref[b, at, :]) * rstd
            n = rstd * (t - jnp.mean(t, axis=-1, keepdims=True) - xh * jnp.mean(t * xh, axis=-1, keepdims=True))
            gi_ref[b, sub, :] = (dy_ref[b, at, :].astype(F32) + n).astype(BF16)

        pltpu.make_async_copy(gi_ref.at[b], gi_out.at[b], store_sem.at[b]).start()

    send_own(0)
    acc_ref[...] = jnp.zeros_like(acc_ref)
    for copy in loads:
        copy.wait()

    @pl.loop(0, batch)
    def _(b):
        @pl.loop(0, nc)
        def _(i):
            @pl.when(i == 0)
            def _():
                arrived(4, b)
                arrived(5, b)

            @pl.when((i == 1) & (b == 0))
            def _():
                service_x(b)
                send_own(1)
                service_dy(b)

            @pl.when(i == 1)
            def _():
                arrived(10, b)
                arrived(11, b)

            @pl.when(i == 2)
            def _():
                arrived(8, b)
                arrived(9, b)

            @pl.when((i == 2) & (b == 1))
            def _():
                ring_second(0)

            @pl.when(i == 3)
            def _():
                service_far(b)

            unit(b, lax.rem(chip + pick(i, GATHER_ORDER), nc))

        dka_ref[...] = jnp.zeros_like(dka_ref)
        dva_ref[...] = jnp.zeros_like(dva_ref)

        @pl.loop(0, 2)
        def _(h):
            attention_head(b, h)

            @pl.when((b == 0) & (h == 0))
            def _():
                service_x(1)

        @pl.when(b == 0)
        def _():
            service_dy(1)

        attention_finish(b)

        @pl.loop(0, nc + 1)
        def _(j):
            @pl.when(j < nc)
            def _():
                input_grad(b, lax.rem(chip + pick(j, SCATTER_ORDER + (0,)), nc))

            for jj in range(nc):
                @pl.when(j == jj)
                def _(jj=jj):
                    to_partner(b, jj, SCATTER_ORDER[jj]).start()

            @pl.when(j > 0)
            def _():
                add_partner(b, j - 1)
                ring_after_partner(b, j - 1)

    for r in range(4):
        gls_ref[r:r + 1, :] = jnp.sum(acc_ref[r], axis=0, keepdims=True)
    gl_ref[me] = gls_ref[...]

    def gl_copy(j, source):
        return pltpu.make_async_remote_copy(
            src_ref=gls_ref, dst_ref=gl_ref.at[source], send_sem=gl_send.at[j], recv_sem=gl_recv.at[j],
            device_id={"tp": lax.rem(me + j, nt)}, device_id_type=MESH_ID)

    for j in range(1, nt):
        gl_copy(j, me).start()

    @pl.loop(0, width, step=BLK)
    def _(i):
        cols = pl.ds(pl.multiple_of(i, BLK), BLK)
        total = dot_tn(m_ref[0, :, cols], dh_ref[0])
        for b in range(1, batch):
            total += dot_tn(m_ref[b, :, cols], dh_ref[b])
        gu_ref[cols, :] = total.astype(BF16)

    ring_second(1)
    stores = [pltpu.make_async_copy(gu_ref, gu_out, store_sem.at[batch])]
    stores[-1].start()

    @pl.loop(0, width, step=BLK)
    def _(i):
        cols = pl.ds(pl.multiple_of(i, BLK), BLK)
        total = dot_tn(u_ref[0], dy_ref[0, :, cols])
        for b in range(1, batch):
            total += dot_tn(u_ref[b], dy_ref[b, :, cols])
        gd_ref[:, cols] = total.astype(BF16)

    stores.append(pltpu.make_async_copy(gd_ref, gd_out, store_sem.at[batch + 1]))
    stores[-1].start()

    @pl.loop(0, width, step=BLK)
    def _(i):
        cols = pl.ds(pl.multiple_of(i, BLK), BLK)
        total = dot_tn(dqkv_ref[0], a_ref[0, :, cols])
        out = dot_nn(ct_ref[0], dy_ref[0, :, cols])
        for b in range(1, batch):
            total += dot_tn(dqkv_ref[b], a_ref[b, :, cols])
            out += dot_nn(ct_ref[b], dy_ref[b, :, cols])
        gq_ref[:, cols] = total.astype(BF16)
        go_ref[:, cols] = out.astype(BF16)

    def store(src, dst):
        stores.append(pltpu.make_async_copy(src, dst, store_sem.at[batch + len(stores)]))
        stores[-1].start()

    store(go_ref, go_out)
    for t, base in ((0, 0), (1, 2 * hd)):
        for part in range(2):
            for g in range(2):
                store(gq_ref.at[pl.ds(base + part * hd + g * hh, hh), :],
                      gq_out.at[pl.ds(g * 3 * hd + t * hd + part * hh, hh), :])
    for g in range(2):
        store(gq_ref.at[pl.ds(4 * hd + g * hd, hd), :], gq_out.at[pl.ds(g * 3 * hd + 2 * hd, hd), :])

    for j in range(1, nt):
        gl_copy(j, lax.rem(me + nt - j, nt)).wait_recv()
    total = gl_ref[0]
    for j in range(1, nt):
        total += gl_ref[j]
    gl_out[...] = total

    finish(0)
    finish(1)

    for b in range(batch):
        pltpu.make_async_copy(gi_ref.at[b], gi_out.at[b], store_sem.at[b]).wait()
        for kind in range(6):
            own(kind, b).wait_send()
        for kind in range(6, 14):
            forward(kind, b).wait_send()
        for j in range(nc):
            to_partner(b, j, SCATTER_ORDER[j]).wait_send()
        for kind in range(4, 10):
            ring(kind, b).wait_send()
    for j in range(1, nt):
        gl_copy(j, me).wait_send()
    for copy in stores:
        copy.wait()


def rope_tables(seq_len, head_dim):
    half_dim = head_dim // 2
    inv_freq = ROPE_BASE ** (-2.0 * jnp.arange(half_dim, dtype=F32) / head_dim)
    angles = jnp.arange(seq_len, dtype=F32)[:, None] * inv_freq[None, :]
    cos, sin = jnp.cos(angles), jnp.sin(angles)
    return jnp.concatenate([cos] * 4, axis=1), jnp.concatenate([-sin, -sin, sin, sin], axis=1)


def solution(mesh):
    act_spec = P('dp', 'tp', None)
    nt = mesh.shape['tp']
    nc = nt // 2

    def device_step(layer_in, grad_out, w_qkv, w_out, w_up, w_down, ln_params):
        batch, rows, width = layer_in.shape
        seq = rows * nt
        groups, _, hd = w_qkv.shape[1:]
        ff = w_up.shape[1]
        wq = jnp.transpose(w_qkv, (1, 2, 3, 0)).reshape(groups * 3 * hd, width)
        wo = w_out.reshape(groups * hd, width)
        cos, sin = rope_tables(seq, hd)
        lanes = groups * hd
        any_spec = pl.BlockSpec(memory_space=pl.ANY)
        vmem_spec = pl.BlockSpec(memory_space=pltpu.VMEM)
        vm = pltpu.VMEM
        dma = pltpu.SemaphoreType.DMA
        outs = pl.pallas_call(
            functools.partial(layer_kernel, nt),
            out_shape=(
                jax.ShapeDtypeStruct((batch, rows, width), BF16),
                jax.ShapeDtypeStruct((groups * 3 * hd, width), BF16),
                jax.ShapeDtypeStruct((lanes, width), BF16),
                jax.ShapeDtypeStruct((width, ff), BF16),
                jax.ShapeDtypeStruct((ff, width), BF16),
                jax.ShapeDtypeStruct((4, width), F32),
            ),
            in_specs=[any_spec] * 6 + [vmem_spec] + [any_spec] * 2,
            out_specs=(any_spec,) * 5 + (vmem_spec,),
            scratch_shapes=[
                vm((batch, seq, width), BF16), vm((batch, seq, width), BF16),
                vm((batch, seq, width), BF16), vm((batch, seq, width), BF16),
                vm((groups * 3 * hd, width), BF16), vm((lanes, width), BF16), vm((width, ff), BF16), vm((ff, width), BF16),
                vm((seq, lanes), F32), vm((seq, lanes), F32),
                vm((batch, seq, lanes), BF16), vm((batch, seq, lanes), BF16), vm((batch, seq, lanes), BF16), vm((batch, seq, lanes), BF16),
                vm((batch, lanes, seq), BF16), vm((batch, lanes, seq), BF16),
                vm((batch, seq, ff), BF16), vm((batch, seq, ff), BF16),
                vm((batch, seq, width), F32), vm((batch, nc, rows, width), F32),
                vm((batch, rows // 2, width), F32), vm((batch, rows // 2, width), F32),
                vm((batch, rows, width), F32), vm((batch, rows, width), F32),
                vm((batch, seq, 1), F32), vm((batch, seq, 1), F32),
                vm((seq, BLK), F32), vm((seq, BLK), F32), vm((seq, seq), BF16), vm((seq, seq), BF16),
                vm((seq, lanes), BF16), vm((seq, lanes), BF16), vm((seq, lanes), F32), vm((seq, lanes), F32),
                vm((lanes, seq), F32), vm((batch, seq, 3 * lanes), BF16), vm((batch, lanes, seq), BF16),
                vm((4, 8, width), F32), vm((nt, 4, width), F32), vm((4, width), F32),
                vm((batch, rows, width), BF16), vm((3 * lanes, width), BF16), vm((lanes, width), BF16), vm((width, ff), BF16), vm((ff, width), BF16),
                dma((17,)), dma((batch + 13,)), dma((batch, 14)), dma((batch, 14)), dma((batch, 10)), dma((batch, 10)), dma((nt,)), dma((nt,)),
            ],
            compiler_params=pltpu.CompilerParams(collective_id=0, has_side_effects=True, vmem_limit_bytes=66000000),
            name="layer_backward",
        )(layer_in, grad_out, wq, wo, w_up, w_down, ln_params, cos, sin)
        grad_in, gq, go, gu, gd, gl = outs
        gq = jnp.transpose(gq.reshape(groups, 3, hd, width), (3, 0, 1, 2))
        return grad_in, gq, go.reshape(w_out.shape), gu, gd, gl

    return jax.shard_map(
        device_step,
        mesh=mesh,
        in_specs=(act_spec, act_spec, P(None, 'tp', None, None), P('tp', None, None, None), P(None, 'tp'), P('tp', None), P(None, None)),
        out_specs=(act_spec, P('dp', 'tp', None, None), P(('dp', 'tp'), None, None, None), P('dp', 'tp'), P(('dp', 'tp'), None), P('dp', None)),
        check_vma=False,
    )
```

profile of v0, /device:TPU:81, one launch (start us, length us, event | category | flops | bytes accessed | tf_op | source)
XLA Modules:
  0.0 113.5 jit_solution(5320990374721257552)
XLA Ops:
  0.6 2.0 %fusion.2 = (f32[1024,32]{1,0:T(8,128)S(1)}, f32[1024,32]{1,0:T(8,128)S(1)}, f32[1024,32]{1,0:T(8,128)S(1)}) fusion(f32[32]{0:T(128)S(1)} %multiply_power_fusion), kind=kLoop, calls=%fused_computation.5 | loop fusion | flops 65536 | bytes 393344 | tf_op jit(solution)/shard_map/neg | solution.py:539
  2.6 1.8 %pad_maximum_fusion = (f32[1024,128]{1,0:T(8,128)}, f32[1024,128]{1,0:T(8,128)}) fusion(f32[1024,32]{1,0:T(8,128)S(1)} %get-tuple-element.26, f32[1024,32]{1,0:T(8,128)S(1)} %get-tuple-element.25, f32[1024,32]{1,0:T(8,128)S(1)} %get-tuple-element.24), kind=kLoop, calls=%fused_computation | loop fusion | flops 786432 | bytes 1441792 | tf_op jit(solution)/shard_map/concatenate | solution.py:539
  4.5 102.0 %layer_backward.1 = (bf16[2,128,1024]{2,1,0:T(8,128)(2,1)}, bf16[384,1024]{1,0:T(8,128)(2,1)}, bf16[128,1024]{1,0:T(8,128)(2,1)}, bf16[1024,512]{1,0:T(8,128)(2,...) custom-call(bf16[2,128,1024]{2,1,0:T(8,128)(2,1)} %x_in.1, bf16[2,128,1024]{2,1,0:T(8,128)(2,1)} %dy_in.1, ...), custom_call_target="tpu_custom_call" | custom-call | tf_op jit(solution)/shard_map/layer_backward/pallas_call | solution.py:560
  106.5 0.0 copy-start.2
  106.5 1.9 %copy.20 = bf16[2,128,1024]{2,1,0:T(8,128)(2,1)} copy(bf16[2,128,1024]{2,1,0:T(8,128)(2,1)} %get-tuple-element.35) | data formatting | bytes 1048576
  108.5 0.0 copy-done.2
  108.5 0.0 copy-start.3
  108.5 0.0 copy-start.1
  108.5 0.9 copy.21
  109.4 0.2 copy-done.3
  109.6 0.7 copy.22
  110.3 0.0 copy-done.1
  110.3 0.0 copy-start
  110.3 1.0 copy.23
  111.2 0.6 copy-done
  111.9 0.0 copy-start.4
  111.9 1.0 copy.24
  112.8 0.0 copy-done.4
  112.8 0.6 copy.25
  (1 shorter events, 0.0 us)
Async XLA Ops:
  106.5 2.0 %copy-start.2 = (bf16[384,1024]{1,0:T(8,128)(2,1)S(1)}, bf16[384,1024]{1,0:T(8,128)(2,1)}, u32[]{:S(2)}) copy-start(bf16[384,1024]{1,0:T(8,128)(2,1)} %get-tuple-element.13) | copy-start | bytes 2359300
  108.5 1.1 copy-start.3
  108.5 1.8 %copy-start.1 = (bf16[1024,512]{1,0:T(8,128)(2,1)S(1)}, bf16[1024,512]{1,0:T(8,128)(2,1)}, u32[]{:S(2)}) copy-start(bf16[1024,512]{1,0:T(8,128)(2,1)} %get-tuple-element.38) | copy-start | bytes 3145732
  110.3 1.6 %copy-start = (bf16[512,1024]{1,0:T(8,128)(2,1)S(1)}, bf16[512,1024]{1,0:T(8,128)(2,1)}, u32[]{:S(2)}) copy-start(bf16[512,1024]{1,0:T(8,128)(2,1)} %get-tuple-element.39) | copy-start | bytes 3145732
  111.9 1.0 copy-start.4
where the time goes:
time: 114 us; the launch traced here: 113 us
  Pallas kernels  102 us (89%)
  local copies, waits for them, and re-layouts  6.92 us (6%)
  other arithmetic  3.82 us (3%)
    pallas_call x1, Pallas kernels, device_step(): pl.pallas_call(functools.partial(layer_kernel, nt), out_shape=(jax.ShapeD...  102 us
    unnamed x16, local copies, waits for them, and re-layouts  6.92 us

commit v1 on v0

--- a/solution.py
+++ b/solution.py
@@ -2,6 +2,7 @@
 
 import jax
 import jax.numpy as jnp
+import numpy as np
 from jax import lax
 from jax.experimental import pallas as pl
 from jax.experimental.pallas import tpu as pltpu
@@ -137,21 +138,25 @@
             source = dev((nc - 1, 1, 2)[(kind - 8) // 2], 1 - core)
         ag(kind, rows_of(ref, b, source), rows_of(ref, b, source), b, partner).wait_recv()
 
-    def send_own(b):
-        for kind in (0, 2, 4, 1, 3, 5):
+    def send_ring(b):
+        for kind in (0, 3, 1, 2):
             own(kind, b).start()
 
-    def service_x(b):
+    def send_partner(b):
+        for kind in (4, 5):
+            own(kind, b).start()
+
+    def service_first(b):
         arrived(0, b)
         forward(6, b).start()
         forward(8, b).start()
-        arrived(2, b)
-        forward(10, b).start()
-
-    def service_dy(b):
         arrived(3, b)
         forward(7, b).start()
         forward(11, b).start()
+
+    def service_second(b):
+        arrived(2, b)
+        forward(10, b).start()
         arrived(1, b)
         forward(9, b).start()
 
@@ -373,45 +378,58 @@
 
         pltpu.make_async_copy(gi_ref.at[b], gi_out.at[b], store_sem.at[b]).start()
 
-    send_own(0)
+    send_ring(0)
+    send_partner(0)
+    send_partner(1)
     acc_ref[...] = jnp.zeros_like(acc_ref)
     for copy in loads:
         copy.wait()
 
     @pl.loop(0, batch)
     def _(b):
-        @pl.loop(0, nc)
+        @pl.loop(b * 2, nc + 1)
         def _(i):
+            step = i - 1
+
             @pl.when(i == 0)
             def _():
-                arrived(4, b)
-                arrived(5, b)
-
-            @pl.when((i == 1) & (b == 0))
-            def _():
-                service_x(b)
-                send_own(1)
-                service_dy(b)
-
-            @pl.when(i == 1)
+                arrived(4, 0)
+                arrived(5, 0)
+
+            @pl.when((step == 0) & (b == 0))
+            def _():
+                arrived(4, 1)
+                arrived(5, 1)
+
+            @pl.when((step == 1) & (b == 0))
+            def _():
+                service_first(0)
+                send_ring(1)
+                service_second(0)
+
+            @pl.when(step == 1)
             def _():
                 arrived(10, b)
                 arrived(11, b)
 
-            @pl.when(i == 2)
+            @pl.when(step == 2)
             def _():
                 arrived(8, b)
                 arrived(9, b)
 
-            @pl.when((i == 2) & (b == 1))
+            @pl.when((step == 2) & (b == 1))
             def _():
                 ring_second(0)
 
-            @pl.when(i == 3)
+            @pl.when(step == 3)
             def _():
                 service_far(b)
 
-            unit(b, lax.rem(chip + pick(i, GATHER_ORDER), nc))
+            unit(jnp.where(step == 0, 1, b), lax.rem(chip + pick(jnp.maximum(step, 0), GATHER_ORDER), nc))
+
+        @pl.when(b == 0)
+        def _():
+            service_first(1)
 
         dka_ref[...] = jnp.zeros_like(dka_ref)
         dva_ref[...] = jnp.zeros_like(dva_ref)
@@ -420,13 +438,9 @@
         def _(h):
             attention_head(b, h)
 
-            @pl.when((b == 0) & (h == 0))
-            def _():
-                service_x(1)
-
         @pl.when(b == 0)
         def _():
-            service_dy(1)
+            service_second(1)
 
         attention_finish(b)
 
@@ -533,10 +547,10 @@
 
 def rope_tables(seq_len, head_dim):
     half_dim = head_dim // 2
-    inv_freq = ROPE_BASE ** (-2.0 * jnp.arange(half_dim, dtype=F32) / head_dim)
-    angles = jnp.arange(seq_len, dtype=F32)[:, None] * inv_freq[None, :]
-    cos, sin = jnp.cos(angles), jnp.sin(angles)
-    return jnp.concatenate([cos] * 4, axis=1), jnp.concatenate([-sin, -sin, sin, sin], axis=1)
+    inv_freq = np.float32(ROPE_BASE) ** (np.float32(-2.0) * np.arange(half_dim, dtype=np.float32) / np.float32(head_dim))
+    angles = np.arange(seq_len, dtype=np.float32)[:, None] * inv_freq[None, :]
+    cos, sin = np.cos(angles), np.sin(angles)
+    return jnp.asarray(np.concatenate([cos] * 4, axis=1)), jnp.asarray(np.concatenate([-sin, -sin, sin, sin], axis=1))
 
 
 def solution(mesh):

time: 114 us -> 98.8 us (0.87)
  Pallas kernels: 102 us -> 91 us
  other arithmetic: 3.82 us -> 0 us
    pallas_call x1, Pallas kernels: 102 us -> 91 us  [device_step(): pl.pallas_call(functools.partial(layer_kernel, nt), out_shape=(jax.ShapeD...]
    neg x1 -> x0, other arithmetic: 1.96 us -> none  [rope_tables(): -sin]
    concatenate x1 -> x0, other arithmetic: 1.85 us -> none  [rope_tables(): jnp.concatenate([cos] * 4, axis=1)]
where the time goes in v1:
time: 98.8 us; the launch traced here: 98.6 us
  Pallas kernels  91 us (92%)
  local copies, waits for them, and re-layouts  6.92 us (7%)
    pallas_call x1, Pallas kernels, device_step(): pl.pallas_call(functools.partial(layer_kernel, nt), out_shape=(jax.ShapeD...  91 us
    unnamed x16, local copies, waits for them, and re-layouts  6.92 us

profile of v1, /device:TPU:81, one launch (start us, length us, event | category | flops | bytes accessed | tf_op | source)
XLA Modules:
  0.0 98.6 jit_solution(17089182183587239166)
XLA Ops:
  0.6 91.0 %layer_backward.1 = (bf16[2,128,1024]{2,1,0:T(8,128)(2,1)}, bf16[384,1024]{1,0:T(8,128)(2,1)}, bf16[128,1024]{1,0:T(8,128)(2,1)}, bf16[1024,512]{1,0:T(8,128)(2,...) custom-call(bf16[2,128,1024]{2,1,0:T(8,128)(2,1)} %x_in.1, bf16[2,128,1024]{2,1,0:T(8,128)(2,1)} %dy_in.1, ...), custom_call_target="tpu_custom_call" | custom-call | tf_op jit(solution)/shard_map/layer_backward/pallas_call | solution.py:574
  91.6 0.0 copy-start.2
  91.6 1.9 %copy.22 = bf16[2,128,1024]{2,1,0:T(8,128)(2,1)} copy(bf16[2,128,1024]{2,1,0:T(8,128)(2,1)} %get-tuple-element.30) | data formatting | bytes 1048576
  93.6 0.0 copy-done.2
  93.6 0.0 copy-start.3
  93.6 0.0 copy-start.1
  93.6 0.9 copy.23
  94.5 0.2 copy-done.3
  94.7 0.7 copy.24
  95.4 0.0 copy-done.1
  95.4 0.0 copy-start
  95.4 1.0 copy.25
  96.3 0.6 copy-done
  97.0 0.0 copy-start.4
  97.0 1.0 copy.26
  97.9 0.0 copy-done.4
  97.9 0.6 copy.27
Async XLA Ops:
  91.6 2.0 %copy-start.2 = (bf16[384,1024]{1,0:T(8,128)(2,1)S(1)}, bf16[384,1024]{1,0:T(8,128)(2,1)}, u32[]{:S(2)}) copy-start(bf16[384,1024]{1,0:T(8,128)(2,1)} %get-tuple-element.13) | copy-start | bytes 2359300
  93.6 1.1 %copy-start.3 = (bf16[128,1024]{1,0:T(8,128)(2,1)S(1)}, bf16[128,1024]{1,0:T(8,128)(2,1)}, u32[]{:S(2)}) copy-start(bf16[128,1024]{1,0:T(8,128)(2,1)} %get-tuple-element.14) | copy-start | bytes 786436
  93.6 1.8 %copy-start.1 = (bf16[1024,512]{1,0:T(8,128)(2,1)S(1)}, bf16[1024,512]{1,0:T(8,128)(2,1)}, u32[]{:S(2)}) copy-start(bf16[1024,512]{1,0:T(8,128)(2,1)} %get-tuple-element.33) | copy-start | bytes 3145732
  95.4 1.6 %copy-start = (bf16[512,1024]{1,0:T(8,128)(2,1)S(1)}, bf16[512,1024]{1,0:T(8,128)(2,1)}, u32[]{:S(2)}) copy-start(bf16[512,1024]{1,0:T(8,128)(2,1)} %get-tuple-element.34) | copy-start | bytes 3145732
  97.0 1.0 copy-start.4

commit v2 on v1

--- a/solution.py
+++ b/solution.py
@@ -86,8 +86,8 @@
         loads[-1].start()
 
     barrier = pltpu.get_barrier_semaphore()
-    for j in range(1, nt):
-        pl.semaphore_signal(barrier, inc=1, device_id={"tp": lax.rem(me + j, nt)}, device_id_type=MESH_ID)
+    for target in (plus, minus, partner):
+        pl.semaphore_signal(barrier, inc=1, device_id={"tp": target}, device_id_type=MESH_ID)
 
     load(x_in, x_ref.at[:, pl.ds(row0(me), rows), :])
     load(dy_in, dy_ref.at[:, pl.ds(row0(me), rows), :])
@@ -104,7 +104,9 @@
     load(wu_in, wu_ref)
     load(wd_in, wd_ref)
 
-    pl.semaphore_wait(barrier, nt - 1)
+    loads[0].wait()
+    loads[1].wait()
+    pl.semaphore_wait(barrier, 3)
 
     def ag(kind, src, dst, b, target):
         return pltpu.make_async_remote_copy(
@@ -115,9 +117,9 @@
         return ref.at[b, pl.ds(row0(device), rows), :]
 
     def own(kind, b):
-        ref, src = ((x_ref, x_in), (dy_ref, dy_in))[kind % 2]
+        ref = (x_ref, dy_ref)[kind % 2]
         target = (plus, minus, partner)[kind // 2]
-        return ag(kind, src.at[b], rows_of(ref, b, me), b, target)
+        return ag(kind, rows_of(ref, b, me), rows_of(ref, b, me), b, target)
 
     def forward(kind, b):
         if kind == 6:
@@ -165,8 +167,6 @@
         forward(12, b).start()
         arrived(7, b)
         forward(13, b).start()
-        arrived(12, b)
-        arrived(13, b)
 
     def rs(kind, src, dst, b, target):
         return pltpu.make_async_remote_copy(
@@ -196,7 +196,7 @@
         return rs(kind, part_rows(b, minus, 1), fm_ref.at[b, hi, :], b, minus)
 
     def add_partner(b, j):
-        off = pick(j, SCATTER_ORDER)
+        off = SCATTER_ORDER[j] if isinstance(j, int) else pick(j, SCATTER_ORDER)
         target = dev(off, core)
         rs(j, part_rows(b, target, None), p_ref.at[b, j], b, partner).wait_recv()
 
@@ -237,8 +237,7 @@
         r0 = pl.multiple_of(cc * pair, pair)
         at = pl.ds(r0, pair)
 
-        @pl.loop(0, pair, step=LN_ROWS)
-        def _(i):
+        for i in range(0, pair, LN_ROWS):
             sub = pl.ds(pl.multiple_of(r0 + i, LN_ROWS), LN_ROWS)
             xs = x_ref[b, sub, :].astype(F32)
             mu = jnp.mean(xs, axis=-1, keepdims=True)
@@ -254,9 +253,10 @@
         dy = dy_ref[b, at, :]
         cos = cos_ref[at, :]
         sin = sin_ref[at, :]
-        q = dot_nt(a, wq_ref[0:2 * hd, :]).astype(BF16).astype(F32)
+        qk = dot_nt(a, wq_ref[0:4 * hd, :]).astype(BF16).astype(F32)
+        q = qk[:, 0:2 * hd]
         q_ref[b, at, :] = (q * cos + pltpu.roll(q, hd, 1) * sin).astype(BF16)
-        k = dot_nt(a, wq_ref[2 * hd:4 * hd, :]).astype(BF16).astype(F32)
+        k = qk[:, 2 * hd:]
         k2 = k * cos + pltpu.roll(k, hd, 1) * sin
         k_ref[b, at, :] = k2.astype(BF16)
         kt_ref[b, :, at] = k2.T.astype(BF16)
@@ -366,7 +366,7 @@
         for kind, ref in ((6, fp_ref), (7, fp_ref), (8, fm_ref), (9, fm_ref)):
             ring(kind, b).wait_recv()
 
-        @pl.loop(0, rows, step=LN_ROWS)
+        @pl.loop(0, rows, step=LN_ROWS, unroll=2)
         def _(i):
             at = pl.ds(pl.multiple_of(me * rows + i, LN_ROWS), LN_ROWS)
             sub = pl.ds(pl.multiple_of(i, LN_ROWS), LN_ROWS)
@@ -382,7 +382,7 @@
     send_partner(0)
     send_partner(1)
     acc_ref[...] = jnp.zeros_like(acc_ref)
-    for copy in loads:
+    for copy in loads[2:]:
         copy.wait()
 
     @pl.loop(0, batch)
@@ -419,11 +419,15 @@
 
             @pl.when((step == 2) & (b == 1))
             def _():
-                ring_second(0)
+                for j in range(1, nc):
+                    add_partner(0, j)
+                    ring_after_partner(0, j)
 
             @pl.when(step == 3)
             def _():
                 service_far(b)
+                arrived(12, b)
+                arrived(13, b)
 
             unit(jnp.where(step == 0, 1, b), lax.rem(chip + pick(jnp.maximum(step, 0), GATHER_ORDER), nc))
 
@@ -437,6 +441,10 @@
         @pl.loop(0, 2)
         def _(h):
             attention_head(b, h)
+
+            @pl.when((b == 1) & (h == 0))
+            def _():
+                ring_second(0)
 
         @pl.when(b == 0)
         def _():
@@ -455,22 +463,28 @@
                 def _(jj=jj):
                     to_partner(b, jj, SCATTER_ORDER[jj]).start()
 
-            @pl.when(j > 0)
-            def _():
-                add_partner(b, j - 1)
-                ring_after_partner(b, j - 1)
+            @pl.when(((j > 0) & (b == 1)) | (j == nc))
+            def _():
+                which = jnp.where(b == 1, j - 1, 0)
+                add_partner(b, which)
+                ring_after_partner(b, which)
 
     for r in range(4):
-        gls_ref[r:r + 1, :] = jnp.sum(acc_ref[r], axis=0, keepdims=True)
-    gl_ref[me] = gls_ref[...]
-
-    def gl_copy(j, source):
+        gls_ref[0, r:r + 1, :] = jnp.sum(acc_ref[r], axis=0, keepdims=True)
+
+    def gl_copy(kind, src, dst, target):
         return pltpu.make_async_remote_copy(
-            src_ref=gls_ref, dst_ref=gl_ref.at[source], send_sem=gl_send.at[j], recv_sem=gl_recv.at[j],
-            device_id={"tp": lax.rem(me + j, nt)}, device_id_type=MESH_ID)
-
-    for j in range(1, nt):
-        gl_copy(j, me).start()
+            src_ref=src, dst_ref=dst, send_sem=gl_send.at[kind], recv_sem=gl_recv.at[kind],
+            device_id={"tp": target}, device_id_type=MESH_ID)
+
+    def from_chip(off):
+        return gl_ref.at[lax.rem(chip + off, nc)]
+
+    gl_pair = gl_copy(0, gls_ref.at[0], gls_ref.at[1], partner)
+    gl_plus = gl_copy(1, from_chip(0), from_chip(0), plus)
+    gl_minus = gl_copy(2, from_chip(0), from_chip(0), minus)
+    gl_far = gl_copy(3, from_chip(nc - 1), from_chip(nc - 1), plus)
+    gl_pair.start()
 
     @pl.loop(0, width, step=BLK)
     def _(i):
@@ -480,7 +494,10 @@
             total += dot_tn(m_ref[b, :, cols], dh_ref[b])
         gu_ref[cols, :] = total.astype(BF16)
 
-    ring_second(1)
+    gl_pair.wait_recv()
+    gl_ref[chip] = gls_ref[0] + gls_ref[1]
+    gl_plus.start()
+    gl_minus.start()
     stores = [pltpu.make_async_copy(gu_ref, gu_out, store_sem.at[batch])]
     stores[-1].start()
 
@@ -519,15 +536,18 @@
     for g in range(2):
         store(gq_ref.at[pl.ds(4 * hd + g * hd, hd), :], gq_out.at[pl.ds(g * 3 * hd + 2 * hd, hd), :])
 
-    for j in range(1, nt):
-        gl_copy(j, lax.rem(me + nt - j, nt)).wait_recv()
+    finish(0)
+    ring_second(1)
+    gl_copy(1, from_chip(nc - 1), from_chip(nc - 1), plus).wait_recv()
+    gl_far.start()
+    finish(1)
+
+    gl_copy(2, from_chip(1), from_chip(1), minus).wait_recv()
+    gl_copy(3, from_chip(2), from_chip(2), plus).wait_recv()
     total = gl_ref[0]
-    for j in range(1, nt):
+    for j in range(1, nc):
         total += gl_ref[j]
     gl_out[...] = total
-
-    finish(0)
-    finish(1)
 
     for b in range(batch):
         pltpu.make_async_copy(gi_ref.at[b], gi_out.at[b], store_sem.at[b]).wait()
@@ -539,8 +559,8 @@
             to_partner(b, j, SCATTER_ORDER[j]).wait_send()
         for kind in range(4, 10):
             ring(kind, b).wait_send()
-    for j in range(1, nt):
-        gl_copy(j, me).wait_send()
+    for copy in (gl_pair, gl_plus, gl_minus, gl_far):
+        copy.wait_send()
     for copy in stores:
         copy.wait()
 
@@ -598,9 +618,9 @@
                 vm((seq, BLK), F32), vm((seq, BLK), F32), vm((seq, seq), BF16), vm((seq, seq), BF16),
                 vm((seq, lanes), BF16), vm((seq, lanes), BF16), vm((seq, lanes), F32), vm((seq, lanes), F32),
                 vm((lanes, seq), F32), vm((batch, seq, 3 * lanes), BF16), vm((batch, lanes, seq), BF16),
-                vm((4, 8, width), F32), vm((nt, 4, width), F32), vm((4, width), F32),
+                vm((4, 8, width), F32), vm((nc, 4, width), F32), vm((2, 4, width), F32),
                 vm((batch, rows, width), BF16), vm((3 * lanes, width), BF16), vm((lanes, width), BF16), vm((width, ff), BF16), vm((ff, width), BF16),
-                dma((17,)), dma((batch + 13,)), dma((batch, 14)), dma((batch, 14)), dma((batch, 10)), dma((batch, 10)), dma((nt,)), dma((nt,)),
+                dma((17,)), dma((batch + 13,)), dma((batch, 14)), dma((batch, 14)), dma((batch, 10)), dma((batch, 10)), dma((4,)), dma((4,)),
             ],
             compiler_params=pltpu.CompilerParams(collective_id=0, has_side_effects=True, vmem_limit_bytes=66000000),
             name="layer_backward",

time: 98.8 us -> 90.3 us (0.914)
  Pallas kernels: 91 us -> 82.5 us
    pallas_call x1, Pallas kernels: 91 us -> 82.5 us  [device_step(): pl.pallas_call(functools.partial(layer_kernel, nt), out_shape=(jax.ShapeD...]
where the time goes in v2:
time: 90.3 us; the launch traced here: 90 us
  Pallas kernels  82.5 us (91%)
  local copies, waits for them, and re-layouts  6.92 us (8%)
    pallas_call x1, Pallas kernels, device_step(): pl.pallas_call(functools.partial(layer_kernel, nt), out_shape=(jax.ShapeD...  82.5 us
    unnamed x16, local copies, waits for them, and re-layouts  6.92 us

profile of v2, /device:TPU:81, one launch (start us, length us, event | category | flops | bytes accessed | tf_op | source)
XLA Modules:
  0.0 90.0 jit_solution(14227165655023302613)
XLA Ops:
  0.6 82.5 %layer_backward.1 = (bf16[2,128,1024]{2,1,0:T(8,128)(2,1)}, bf16[384,1024]{1,0:T(8,128)(2,1)}, bf16[128,1024]{1,0:T(8,128)(2,1)}, bf16[1024,512]{1,0:T(8,128)(2,...) custom-call(bf16[2,128,1024]{2,1,0:T(8,128)(2,1)} %x_in.1, bf16[2,128,1024]{2,1,0:T(8,128)(2,1)} %dy_in.1, ...), custom_call_target="tpu_custom_call" | custom-call | tf_op jit(solution)/shard_map/layer_backward/pallas_call | solution.py:594
  83.1 0.0 copy-start.2
  83.1 1.9 %copy.22 = bf16[2,128,1024]{2,1,0:T(8,128)(2,1)} copy(bf16[2,128,1024]{2,1,0:T(8,128)(2,1)} %get-tuple-element.30) | data formatting | bytes 1048576
  85.1 0.0 copy-done.2
  85.1 0.0 copy-start.3
  85.1 0.0 copy-start.1
  85.1 0.9 copy.23
  85.9 0.2 copy-done.3
  86.2 0.7 copy.24
  86.9 0.0 copy-done.1
  86.9 0.0 copy-start
  86.9 1.0 %copy.25 = bf16[1024,512]{1,0:T(8,128)(2,1)} copy(bf16[1024,512]{1,0:T(8,128)(2,1)S(1)} %copy-done.1) | data formatting | bytes 2097152
  87.8 0.6 copy-done
  88.5 0.0 copy-start.4
  88.5 1.0 %copy.26 = bf16[512,1024]{1,0:T(8,128)(2,1)} copy(bf16[512,1024]{1,0:T(8,128)(2,1)S(1)} %copy-done) | data formatting | bytes 2097152
  89.4 0.0 copy-done.4
  89.4 0.6 copy.27
Async XLA Ops:
  83.1 2.0 %copy-start.2 = (bf16[384,1024]{1,0:T(8,128)(2,1)S(1)}, bf16[384,1024]{1,0:T(8,128)(2,1)}, u32[]{:S(2)}) copy-start(bf16[384,1024]{1,0:T(8,128)(2,1)} %get-tuple-element.13) | copy-start | bytes 2359300
  85.1 1.1 %copy-start.3 = (bf16[128,1024]{1,0:T(8,128)(2,1)S(1)}, bf16[128,1024]{1,0:T(8,128)(2,1)}, u32[]{:S(2)}) copy-start(bf16[128,1024]{1,0:T(8,128)(2,1)} %get-tuple-element.14) | copy-start | bytes 786436
  85.1 1.8 %copy-start.1 = (bf16[1024,512]{1,0:T(8,128)(2,1)S(1)}, bf16[1024,512]{1,0:T(8,128)(2,1)}, u32[]{:S(2)}) copy-start(bf16[1024,512]{1,0:T(8,128)(2,1)} %get-tuple-element.33) | copy-start | bytes 3145732
  86.9 1.6 %copy-start = (bf16[512,1024]{1,0:T(8,128)(2,1)S(1)}, bf16[512,1024]{1,0:T(8,128)(2,1)}, u32[]{:S(2)}) copy-start(bf16[512,1024]{1,0:T(8,128)(2,1)} %get-tuple-element.34) | copy-start | bytes 3145732
  88.5 1.0 %copy-start.4 = (f32[4,1024]{1,0:T(4,128)S(1)}, f32[4,1024]{1,0:T(4,128)}, u32[]{:S(2)}) copy-start(f32[4,1024]{1,0:T(4,128)} %get-tuple-element.35) | copy-start | bytes 49156

commit v3 on v2

--- a/solution.py
+++ b/solution.py
@@ -19,6 +19,7 @@
 MESH_ID = pl.DeviceIdType.MESH
 BLK = 256
 LN_ROWS = 32
+VMEM_LIMIT = 62000000
 GATHER_ORDER = (0, 1, 3, 2)
 SCATTER_ORDER = (2, 1, 3, 0)
 
@@ -48,13 +49,12 @@
 
 
 def layer_kernel(nt, x_in, dy_in, wq_in, wo_in, wu_in, wd_in, ln_ref, cos_in, sin_in,
-                 gi_out, gq_out, go_out, gu_out, gd_out, gl_out,
+                 gi_ref, gq_ref, go_ref, gu_ref, gd_ref, gl_out,
                  x_ref, dy_ref, a_ref, m_ref, wq_ref, wo_ref, wu_ref, wd_ref, cos_ref, sin_ref,
                  q_ref, k_ref, v_ref, dc_ref, kt_ref, vt_ref, u_ref, dh_ref, t_ref, p_ref,
                  hp_ref, hm_ref, fp_ref, fm_ref, mu_ref, rstd_ref, s_ref, dp_ref, pt_ref, ds_ref,
                  qm_ref, dcm_ref, dka_ref, dva_ref, dqt_ref, dqkv_ref, ct_ref, acc_ref, gl_ref, gls_ref,
-                 gi_ref, gq_ref, go_ref, gu_ref, gd_ref,
-                 load_sem, store_sem, ag_send, ag_recv, rs_send, rs_recv, gl_send, gl_recv):
+                 load_sem, ag_send, ag_recv, rs_send, rs_recv, gl_send, gl_recv):
     nc = nt // 2
     batch, seq, width = x_ref.shape
     ff = wu_ref.shape[1]
@@ -376,8 +376,6 @@
             n = rstd * (t - jnp.mean(t, axis=-1, keepdims=True) - xh * jnp.mean(t * xh, axis=-1, keepdims=True))
             gi_ref[b, sub, :] = (dy_ref[b, at, :].astype(F32) + n).astype(BF16)
 
-        pltpu.make_async_copy(gi_ref.at[b], gi_out.at[b], store_sem.at[b]).start()
-
     send_ring(0)
     send_partner(0)
     send_partner(1)
@@ -498,8 +496,6 @@
     gl_ref[chip] = gls_ref[0] + gls_ref[1]
     gl_plus.start()
     gl_minus.start()
-    stores = [pltpu.make_async_copy(gu_ref, gu_out, store_sem.at[batch])]
-    stores[-1].start()
 
     @pl.loop(0, width, step=BLK)
     def _(i):
@@ -508,9 +504,6 @@
         for b in range(1, batch):
             total += dot_tn(u_ref[b], dy_ref[b, :, cols])
         gd_ref[:, cols] = total.astype(BF16)
-
-    stores.append(pltpu.make_async_copy(gd_ref, gd_out, store_sem.at[batch + 1]))
-    stores[-1].start()
 
     @pl.loop(0, width, step=BLK)
     def _(i):
@@ -520,21 +513,16 @@
         for b in range(1, batch):
             total += dot_tn(dqkv_ref[b], a_ref[b, :, cols])
             out += dot_nn(ct_ref[b], dy_ref[b, :, cols])
-        gq_ref[:, cols] = total.astype(BF16)
+        total = total.astype(BF16)
+        for t, base in ((0, 0), (1, 2 * hd)):
+            for part in range(2):
+                for g in range(2):
+                    row, to = base + part * hd + g * hh, g * 3 * hd + t * hd + part * hh
+                    gq_ref[to:to + hh, cols] = total[row:row + hh]
+        for g in range(2):
+            row, to = 4 * hd + g * hd, g * 3 * hd + 2 * hd
+            gq_ref[to:to + hd, cols] = total[row:row + hd]
         go_ref[:, cols] = out.astype(BF16)
-
-    def store(src, dst):
-        stores.append(pltpu.make_async_copy(src, dst, store_sem.at[batch + len(stores)]))
-        stores[-1].start()
-
-    store(go_ref, go_out)
-    for t, base in ((0, 0), (1, 2 * hd)):
-        for part in range(2):
-            for g in range(2):
-                store(gq_ref.at[pl.ds(base + part * hd + g * hh, hh), :],
-                      gq_out.at[pl.ds(g * 3 * hd + t * hd + part * hh, hh), :])
-    for g in range(2):
-        store(gq_ref.at[pl.ds(4 * hd + g * hd, hd), :], gq_out.at[pl.ds(g * 3 * hd + 2 * hd, hd), :])
 
     finish(0)
     ring_second(1)
@@ -550,7 +538,6 @@
     gl_out[...] = total
 
     for b in range(batch):
-        pltpu.make_async_copy(gi_ref.at[b], gi_out.at[b], store_sem.at[b]).wait()
         for kind in range(6):
             own(kind, b).wait_send()
         for kind in range(6, 14):
@@ -561,7 +548,14 @@
             ring(kind, b).wait_send()
     for copy in (gl_pair, gl_plus, gl_minus, gl_far):
         copy.wait_send()
-    for copy in stores:
+
+
+def store_kernel(*refs):
+    n = len(refs) // 2
+    copies = [pltpu.make_async_copy(refs[i], refs[n + i], refs[2 * n].at[i]) for i in range(n)]
+    for copy in copies:
+        copy.start()
+    for copy in copies:
         copy.wait()
 
 
@@ -591,18 +585,19 @@
         vmem_spec = pl.BlockSpec(memory_space=pltpu.VMEM)
         vm = pltpu.VMEM
         dma = pltpu.SemaphoreType.DMA
+        shapes = (
+            jax.ShapeDtypeStruct((batch, rows, width), BF16),
+            jax.ShapeDtypeStruct((groups * 3 * hd, width), BF16),
+            jax.ShapeDtypeStruct((lanes, width), BF16),
+            jax.ShapeDtypeStruct((width, ff), BF16),
+            jax.ShapeDtypeStruct((ff, width), BF16),
+            jax.ShapeDtypeStruct((4, width), F32),
+        )
         outs = pl.pallas_call(
             functools.partial(layer_kernel, nt),
-            out_shape=(
-                jax.ShapeDtypeStruct((batch, rows, width), BF16),
-                jax.ShapeDtypeStruct((groups * 3 * hd, width), BF16),
-                jax.ShapeDtypeStruct((lanes, width), BF16),
-                jax.ShapeDtypeStruct((width, ff), BF16),
-                jax.ShapeDtypeStruct((ff, width), BF16),
-                jax.ShapeDtypeStruct((4, width), F32),
-            ),
+            out_shape=tuple(vm(shape.shape, shape.dtype) for shape in shapes),
             in_specs=[any_spec] * 6 + [vmem_spec] + [any_spec] * 2,
-            out_specs=(any_spec,) * 5 + (vmem_spec,),
+            out_specs=(vmem_spec,) * 6,
             scratch_shapes=[
                 vm((batch, seq, width), BF16), vm((batch, seq, width), BF16),
                 vm((batch, seq, width), BF16), vm((batch, seq, width), BF16),
@@ -619,12 +614,20 @@
                 vm((seq, lanes), BF16), vm((seq, lanes), BF16), vm((seq, lanes), F32), vm((seq, lanes), F32),
                 vm((lanes, seq), F32), vm((batch, seq, 3 * lanes), BF16), vm((batch, lanes, seq), BF16),
                 vm((4, 8, width), F32), vm((nc, 4, width), F32), vm((2, 4, width), F32),
-                vm((batch, rows, width), BF16), vm((3 * lanes, width), BF16), vm((lanes, width), BF16), vm((width, ff), BF16), vm((ff, width), BF16),
-                dma((17,)), dma((batch + 13,)), dma((batch, 14)), dma((batch, 14)), dma((batch, 10)), dma((batch, 10)), dma((4,)), dma((4,)),
+                dma((17,)), dma((batch, 14)), dma((batch, 14)), dma((batch, 10)), dma((batch, 10)), dma((4,)), dma((4,)),
             ],
-            compiler_params=pltpu.CompilerParams(collective_id=0, has_side_effects=True, vmem_limit_bytes=66000000),
+            compiler_params=pltpu.CompilerParams(collective_id=0, has_side_effects=True, vmem_limit_bytes=VMEM_LIMIT),
             name="layer_backward",
         )(layer_in, grad_out, wq, wo, w_up, w_down, ln_params, cos, sin)
+        outs = pl.pallas_call(
+            store_kernel,
+            out_shape=shapes,
+            in_specs=[vmem_spec] * 6,
+            out_specs=(any_spec,) * 6,
+            scratch_shapes=[dma((6,))],
+            compiler_params=pltpu.CompilerParams(vmem_limit_bytes=1 << 20),
+            name="store_outputs",
+        )(*(pltpu.with_memory_space_constraint(out, pltpu.VMEM) for out in outs))
         grad_in, gq, go, gu, gd, gl = outs
         gq = jnp.transpose(gq.reshape(groups, 3, hd, width), (3, 0, 1, 2))
         return grad_in, gq, go.reshape(w_out.shape), gu, gd, gl

time: 90.3 us -> 83.8 us (0.928)
  local copies, waits for them, and re-layouts: 6.92 us -> 0 us
    unnamed x16 -> x0, local copies, waits for them, and re-layouts: 6.92 us -> none
    pallas_call x1 -> x2, Pallas kernels: 82.5 us -> 82.9 us  [the longest x1 81.1 us: device_step(): pl.pallas_call(functools.partial(layer_kernel, nt), out_shape=tuple((vm(s...]
where the time goes in v3:
time: 83.8 us; the launch traced here: 83.6 us
  Pallas kernels  82.9 us (99%)
    pallas_call x1, Pallas kernels, device_step(): pl.pallas_call(functools.partial(layer_kernel, nt), out_shape=tuple((vm(s...  81.1 us
    pallas_call x1, Pallas kernels, device_step(): pl.pallas_call(store_kernel, out_shape=shapes, in_specs=[vmem_spec] * 6,...  1.89 us

profile of v3, /device:TPU:81, one launch (start us, length us, event | category | flops | bytes accessed | tf_op | source)
XLA Modules:
  0.0 83.6 jit_solution(14581071222831205351)
XLA Ops:
  0.6 81.1 %layer_backward.1 = (bf16[2,128,1024]{2,1,0:T(8,128)(2,1)S(1)}, bf16[384,1024]{1,0:T(8,128)(2,1)S(1)}, bf16[128,1024]{1,0:T(8,128)(2,1)S(1)}, bf16[1024,512]{1,0...) custom-call(bf16[2,128,1024]{2,1,0:T(8,128)(2,1)} %x_in.1, bf16[2,128,1024]{2,1,0:T(8,128)(2,1)} %dy_in.1, ...), custom_call_target="tpu_custom_call" | custom-call | tf_op jit(solution)/shard_map/layer_backward/pallas_call | solution.py:596
  81.7 1.9 %store_outputs.1 = (bf16[2,128,1024]{2,1,0:T(8,128)(2,1)}, bf16[384,1024]{1,0:T(8,128)(2,1)}, bf16[128,1024]{1,0:T(8,128)(2,1)}, bf16[1024,512]{1,0:T(8,128)(2,1...) custom-call(bf16[2,128,1024]{2,1,0:T(8,128)(2,1)S(1)} %get-tuple-element.18.refs_0_, ...), custom_call_target="tpu_custom_call" | custom-call | tf_op jit(solution)/shard_map/store_outputs/pallas_call | solution.py:622

commit v4 on v3

--- a/solution.py
+++ b/solution.py
@@ -60,6 +60,7 @@
     ff = wu_ref.shape[1]
     rows = x_in.shape[1]
     half = rows // 2
+    quarter = rows // 4
     pair = 2 * rows
     hd = wo_in.shape[0] // 2
     hh = hd // 2
@@ -91,19 +92,6 @@
 
     load(x_in, x_ref.at[:, pl.ds(row0(me), rows), :])
     load(dy_in, dy_ref.at[:, pl.ds(row0(me), rows), :])
-    for t, base in ((0, 0), (1, 2 * hd)):
-        for part in range(2):
-            for g in range(2):
-                load(wq_in.at[pl.ds(g * 3 * hd + t * hd + part * hh, hh), :],
-                     wq_ref.at[pl.ds(base + part * hd + g * hh, hh), :])
-    for g in range(2):
-        load(wq_in.at[pl.ds(g * 3 * hd + 2 * hd, hd), :], wq_ref.at[pl.ds(4 * hd + g * hd, hd), :])
-    load(cos_in, cos_ref)
-    load(sin_in, sin_ref)
-    load(wo_in, wo_ref)
-    load(wu_in, wu_ref)
-    load(wd_in, wd_ref)
-
     loads[0].wait()
     loads[1].wait()
     pl.semaphore_wait(barrier, 3)
@@ -173,65 +161,45 @@
             src_ref=src, dst_ref=dst, send_sem=rs_send.at[b, kind], recv_sem=rs_recv.at[b, kind],
             device_id={"tp": target}, device_id_type=MESH_ID)
 
-    def part_rows(b, device, part):
-        if part is None:
-            return t_ref.at[b, pl.ds(row0(device), rows), :]
-        return t_ref.at[b, pl.ds(pl.multiple_of(device * rows + part * half, half), half), :]
+    def part_rows(b, device, first, count):
+        return t_ref.at[b, pl.ds(pl.multiple_of(device * rows + first, quarter), count), :]
 
     def to_partner(b, j, off):
-        return rs(j, part_rows(b, dev(off, 1 - core), None), p_ref.at[b, j], b, partner)
+        return rs(j, part_rows(b, dev(off, 1 - core), 0, rows), p_ref.at[b, j], b, partner)
 
     def ring(kind, b):
-        lo, hi = pl.ds(0, half), pl.ds(half, half)
-        if kind == 4:
-            return rs(kind, part_rows(b, dev(2, core), 0), hp_ref.at[b], b, plus)
-        if kind == 5:
-            return rs(kind, part_rows(b, dev(2, core), 1), hm_ref.at[b], b, minus)
-        if kind == 6:
-            return rs(kind, part_rows(b, plus, 1), fp_ref.at[b, hi, :], b, plus)
-        if kind == 7:
-            return rs(kind, part_rows(b, plus, 0), fp_ref.at[b, lo, :], b, plus)
-        if kind == 8:
-            return rs(kind, part_rows(b, minus, 0), fm_ref.at[b, lo, :], b, minus)
-        return rs(kind, part_rows(b, minus, 1), fm_ref.at[b, hi, :], b, minus)
+        if kind < 6:
+            to, ref = ((plus, hp_ref), (minus, hm_ref))[kind - 4]
+            return rs(kind, part_rows(b, dev(2, core), (kind - 4) * half, half), ref.at[b], b, to)
+        to, ref, first, count = {
+            6: (plus, fp_ref, half, half), 7: (plus, fp_ref, 0, quarter), 10: (plus, fp_ref, quarter, quarter),
+            8: (minus, fm_ref, 0, half), 9: (minus, fm_ref, half, quarter), 11: (minus, fm_ref, half + quarter, quarter),
+        }[kind]
+        return rs(kind, part_rows(b, to, first, count), ref.at[b, pl.ds(first, count), :], b, to)
 
     def add_partner(b, j):
-        off = SCATTER_ORDER[j] if isinstance(j, int) else pick(j, SCATTER_ORDER)
-        target = dev(off, core)
-        rs(j, part_rows(b, target, None), p_ref.at[b, j], b, partner).wait_recv()
+        target = dev(SCATTER_ORDER[j], core)
+        rs(j, part_rows(b, target, 0, rows), p_ref.at[b, j], b, partner).wait_recv()
 
         @pl.loop(0, rows, step=LN_ROWS)
         def _(i):
             at = pl.ds(pl.multiple_of(target * rows + i, LN_ROWS), LN_ROWS)
             t_ref[b, at, :] += p_ref[b, j, pl.ds(pl.multiple_of(i, LN_ROWS), LN_ROWS), :]
 
-    def ring_after_partner(b, j):
-        @pl.when(j == 0)
-        def _():
-            ring(4, b).start()
-            ring(5, b).start()
-
-        @pl.when(j == 1)
-        def _():
-            ring(6, b).start()
-
-        @pl.when(j == 2)
-        def _():
-            ring(8, b).start()
-
-    def add_half(b, device, part, ref):
-        @pl.loop(0, half, step=LN_ROWS)
-        def _(i):
-            at = pl.ds(pl.multiple_of(device * rows + part * half + i, LN_ROWS), LN_ROWS)
-            t_ref[b, at, :] += ref[b, pl.ds(pl.multiple_of(i, LN_ROWS), LN_ROWS), :]
+    def add_quarter(b, device, first, ref, at):
+        t_ref[b, pl.ds(pl.multiple_of(device * rows + first, quarter), quarter), :] += ref[b, pl.ds(at, quarter), :]
 
     def ring_second(b):
         ring(4, b).wait_recv()
-        add_half(b, plus, 0, hp_ref)
+        add_quarter(b, plus, 0, hp_ref, 0)
         ring(7, b).start()
         ring(5, b).wait_recv()
-        add_half(b, minus, 1, hm_ref)
+        add_quarter(b, minus, half, hm_ref, 0)
         ring(9, b).start()
+        add_quarter(b, plus, quarter, hp_ref, quarter)
+        ring(10, b).start()
+        add_quarter(b, minus, half + quarter, hm_ref, quarter)
+        ring(11, b).start()
 
     def unit(b, cc):
         r0 = pl.multiple_of(cc * pair, pair)
@@ -337,20 +305,15 @@
             dva_ref[ks, :] += dot_nn(pt_ref[ks, kb * BLK:], dcm_ref[kb * BLK:, :])
             dka_ref[ks, :] += dot_nn(ds_ref[ks, kb * BLK:], qm_ref[kb * BLK:, :])
 
-    def attention_finish(b):
-        @pl.loop(0, seq, step=BLK)
-        def _(i):
-            at = pl.ds(pl.multiple_of(i, BLK), BLK)
-            cos = cos_ref[at, :]
-            sin = sin_ref[at, :]
-            dq = dqt_ref[:, at].T
-            dqkv_ref[b, at, 0:2 * hd] = (dq * cos - pltpu.roll(dq, hd, 1) * sin).astype(BF16)
-            dk = dka_ref[at, :]
-            dqkv_ref[b, at, 2 * hd:4 * hd] = (dk * cos - pltpu.roll(dk, hd, 1) * sin).astype(BF16)
-            dqkv_ref[b, at, 4 * hd:6 * hd] = dva_ref[at, :].astype(BF16)
-
     def input_grad(b, cc):
         at = pl.ds(pl.multiple_of(cc * pair, pair), pair)
+        cos = cos_ref[at, :]
+        sin = sin_ref[at, :]
+        dq = dqt_ref[:, at].T
+        dqkv_ref[b, at, 0:2 * hd] = (dq * cos - pltpu.roll(dq, hd, 1) * sin).astype(BF16)
+        dk = dka_ref[at, :]
+        dqkv_ref[b, at, 2 * hd:4 * hd] = (dk * cos - pltpu.roll(dk, hd, 1) * sin).astype(BF16)
+        dqkv_ref[b, at, 4 * hd:6 * hd] = dva_ref[at, :].astype(BF16)
         dqkv = dqkv_ref[b, at, :]
         mu = mu_ref[b, at, :]
         rstd = rstd_ref[b, at, :]
@@ -362,23 +325,55 @@
             acc_ref[0, :, cols] += fold8(da * xh)
             acc_ref[1, :, cols] += fold8(da)
 
+    def finish_rows(b, first):
+        at = pl.ds(pl.multiple_of(me * rows + first, quarter), quarter)
+        sub = pl.ds(first, quarter)
+        t = t_ref[b, at, :] + fp_ref[b, sub, :] + fm_ref[b, sub, :]
+        rstd = rstd_ref[b, at, :]
+        xh = (x_ref[b, at, :].astype(F32) - mu_ref[b, at, :]) * rstd
+        n = rstd * (t - jnp.mean(t, axis=-1, keepdims=True) - xh * jnp.mean(t * xh, axis=-1, keepdims=True))
+        gi_ref[b, sub, :] = (dy_ref[b, at, :].astype(F32) + n).astype(BF16)
+
     def finish(b):
-        for kind, ref in ((6, fp_ref), (7, fp_ref), (8, fm_ref), (9, fm_ref)):
+        for kind in (6, 8, 7, 9):
             ring(kind, b).wait_recv()
-
-        @pl.loop(0, rows, step=LN_ROWS, unroll=2)
-        def _(i):
-            at = pl.ds(pl.multiple_of(me * rows + i, LN_ROWS), LN_ROWS)
-            sub = pl.ds(pl.multiple_of(i, LN_ROWS), LN_ROWS)
-            t = t_ref[b, at, :] + fp_ref[b, sub, :] + fm_ref[b, sub, :]
-            rstd = rstd_ref[b, at, :]
-            xh = (x_ref[b, at, :].astype(F32) - mu_ref[b, at, :]) * rstd
-            n = rstd * (t - jnp.mean(t, axis=-1, keepdims=True) - xh * jnp.mean(t * xh, axis=-1, keepdims=True))
-            gi_ref[b, sub, :] = (dy_ref[b, at, :].astype(F32) + n).astype(BF16)
+        finish_rows(b, 0)
+        finish_rows(b, half)
+        for kind in (10, 11):
+            ring(kind, b).wait_recv()
+        finish_rows(b, quarter)
+        finish_rows(b, half + quarter)
+
+    def gl_copy(kind, src, dst, target):
+        return pltpu.make_async_remote_copy(
+            src_ref=src, dst_ref=dst, send_sem=gl_send.at[kind], recv_sem=gl_recv.at[kind],
+            device_id={"tp": target}, device_id_type=MESH_ID)
+
+    def from_chip(off):
+        return gl_ref.at[lax.rem(chip + off, nc)]
+
+    gl_pair = gl_copy(0, gls_ref.at[0], gls_ref.at[1], partner)
+    gl_plus = gl_copy(1, from_chip(0), from_chip(0), plus)
+    gl_minus = gl_copy(2, from_chip(0), from_chip(0), minus)
+    gl_far = gl_copy(3, from_chip(nc - 1), from_chip(nc - 1), plus)
 
     send_ring(0)
     send_partner(0)
     send_partner(1)
+
+    for t, base in ((0, 0), (1, 2 * hd)):
+        for part in range(2):
+            for g in range(2):
+                load(wq_in.at[pl.ds(g * 3 * hd + t * hd + part * hh, hh), :],
+                     wq_ref.at[pl.ds(base + part * hd + g * hh, hh), :])
+    for g in range(2):
+        load(wq_in.at[pl.ds(g * 3 * hd + 2 * hd, hd), :], wq_ref.at[pl.ds(4 * hd + g * hd, hd), :])
+    load(cos_in, cos_ref)
+    load(sin_in, sin_ref)
+    load(wo_in, wo_ref)
+    load(wu_in, wu_ref)
+    load(wd_in, wd_ref)
+
     acc_ref[...] = jnp.zeros_like(acc_ref)
     for copy in loads[2:]:
         copy.wait()
@@ -417,9 +412,11 @@
 
             @pl.when((step == 2) & (b == 1))
             def _():
-                for j in range(1, nc):
-                    add_partner(0, j)
-                    ring_after_partner(0, j)
+                add_partner(0, 1)
+                ring(6, 0).start()
+                add_partner(0, 2)
+                ring(8, 0).start()
+                add_partner(0, 3)
 
             @pl.when(step == 3)
             def _():
@@ -433,6 +430,10 @@
         def _():
             service_first(1)
 
+        @pl.when(b == 1)
+        def _():
+            ring_second(0)
+
         dka_ref[...] = jnp.zeros_like(dka_ref)
         dva_ref[...] = jnp.zeros_like(dva_ref)
 
@@ -440,49 +441,36 @@
         def _(h):
             attention_head(b, h)
 
-            @pl.when((b == 1) & (h == 0))
-            def _():
-                ring_second(0)
-
         @pl.when(b == 0)
         def _():
             service_second(1)
 
-        attention_finish(b)
-
-        @pl.loop(0, nc + 1)
+        @pl.loop(0, nc)
         def _(j):
-            @pl.when(j < nc)
-            def _():
-                input_grad(b, lax.rem(chip + pick(j, SCATTER_ORDER + (0,)), nc))
-
+            input_grad(b, lax.rem(chip + pick(j, SCATTER_ORDER), nc))
             for jj in range(nc):
                 @pl.when(j == jj)
                 def _(jj=jj):
                     to_partner(b, jj, SCATTER_ORDER[jj]).start()
 
-            @pl.when(((j > 0) & (b == 1)) | (j == nc))
-            def _():
-                which = jnp.where(b == 1, j - 1, 0)
-                add_partner(b, which)
-                ring_after_partner(b, which)
+            @pl.when(j == 3 - b)
+            def _():
+                add_partner(b, 0)
+                ring(4, b).start()
+                ring(5, b).start()
 
     for r in range(4):
         gls_ref[0, r:r + 1, :] = jnp.sum(acc_ref[r], axis=0, keepdims=True)
-
-    def gl_copy(kind, src, dst, target):
-        return pltpu.make_async_remote_copy(
-            src_ref=src, dst_ref=dst, send_sem=gl_send.at[kind], recv_sem=gl_recv.at[kind],
-            device_id={"tp": target}, device_id_type=MESH_ID)
-
-    def from_chip(off):
-        return gl_ref.at[lax.rem(chip + off, nc)]
-
-    gl_pair = gl_copy(0, gls_ref.at[0], gls_ref.at[1], partner)
-    gl_plus = gl_copy(1, from_chip(0), from_chip(0), plus)
-    gl_minus = gl_copy(2, from_chip(0), from_chip(0), minus)
-    gl_far = gl_copy(3, from_chip(nc - 1), from_chip(nc - 1), plus)
     gl_pair.start()
+    add_partner(1, 1)
+    add_partner(1, 2)
+    gl_pair.wait_recv()
+    gl_ref[chip] = gls_ref[0] + gls_ref[1]
+    gl_plus.start()
+    gl_minus.start()
+    ring(6, 1).start()
+    ring(8, 1).start()
+    add_partner(1, 3)
 
     @pl.loop(0, width, step=BLK)
     def _(i):
@@ -492,10 +480,6 @@
             total += dot_tn(m_ref[b, :, cols], dh_ref[b])
         gu_ref[cols, :] = total.astype(BF16)
 
-    gl_pair.wait_recv()
-    gl_ref[chip] = gls_ref[0] + gls_ref[1]
-    gl_plus.start()
-    gl_minus.start()
 
     @pl.loop(0, width, step=BLK)
     def _(i):
@@ -504,6 +488,10 @@
         for b in range(1, batch):
             total += dot_tn(u_ref[b], dy_ref[b, :, cols])
         gd_ref[:, cols] = total.astype(BF16)
+
+    gl_copy(1, from_chip(nc - 1), from_chip(nc - 1), plus).wait_recv()
+    gl_far.start()
+    ring_second(1)
 
     @pl.loop(0, width, step=BLK)
     def _(i):
@@ -525,11 +513,6 @@
         go_ref[:, cols] = out.astype(BF16)
 
     finish(0)
-    ring_second(1)
-    gl_copy(1, from_chip(nc - 1), from_chip(nc - 1), plus).wait_recv()
-    gl_far.start()
-    finish(1)
-
     gl_copy(2, from_chip(1), from_chip(1), minus).wait_recv()
     gl_copy(3, from_chip(2), from_chip(2), plus).wait_recv()
     total = gl_ref[0]
@@ -544,10 +527,15 @@
             forward(kind, b).wait_send()
         for j in range(nc):
             to_partner(b, j, SCATTER_ORDER[j]).wait_send()
-        for kind in range(4, 10):
-            ring(kind, b).wait_send()
+    for kind in range(4, 12):
+        ring(kind, 0).wait_send()
+    for kind in (4, 5, 6, 8):
+        ring(kind, 1).wait_send()
     for copy in (gl_pair, gl_plus, gl_minus, gl_far):
         copy.wait_send()
+    finish(1)
+    for kind in (7, 9, 10, 11):
+        ring(kind, 1).wait_send()
 
 
 def store_kernel(*refs):
@@ -614,7 +602,7 @@
                 vm((seq, lanes), BF16), vm((seq, lanes), BF16), vm((seq, lanes), F32), vm((seq, lanes), F32),
                 vm((lanes, seq), F32), vm((batch, seq, 3 * lanes), BF16), vm((batch, lanes, seq), BF16),
                 vm((4, 8, width), F32), vm((nc, 4, width), F32), vm((2, 4, width), F32),
-                dma((17,)), dma((batch, 14)), dma((batch, 14)), dma((batch, 10)), dma((batch, 10)), dma((4,)), dma((4,)),
+                dma((17,)), dma((batch, 14)), dma((batch, 14)), dma((batch, 12)), dma((batch, 12)), dma((4,)), dma((4,)),
             ],
             compiler_params=pltpu.CompilerParams(collective_id=0, has_side_effects=True, vmem_limit_bytes=VMEM_LIMIT),
             name="layer_backward",

time: 83.8 us -> 81.3 us (0.970)
  Pallas kernels: 82.9 us -> 80.5 us
    pallas_call x1, Pallas kernels: 81.1 us -> 78.6 us  [device_step(): pl.pallas_call(functools.partial(layer_kernel, nt), out_shape=tuple((vm(s...]
where the time goes in v4:
time: 81.3 us; the launch traced here: 81.1 us
  Pallas kernels  80.5 us (99%)
    pallas_call x1, Pallas kernels, device_step(): pl.pallas_call(functools.partial(layer_kernel, nt), out_shape=tuple((vm(s...  78.6 us
    pallas_call x1, Pallas kernels, device_step(): pl.pallas_call(store_kernel, out_shape=shapes, in_specs=[vmem_spec] * 6,...  1.89 us

profile of v4, /device:TPU:81, one launch (start us, length us, event | category | flops | bytes accessed | tf_op | source)
XLA Modules:
  0.0 81.1 jit_solution(17236950605794928190)
XLA Ops:
  0.6 78.6 %layer_backward.1 = (bf16[2,128,1024]{2,1,0:T(8,128)(2,1)S(1)}, bf16[384,1024]{1,0:T(8,128)(2,1)S(1)}, bf16[128,1024]{1,0:T(8,128)(2,1)S(1)}, bf16[1024,512]{1,0...) custom-call(bf16[2,128,1024]{2,1,0:T(8,128)(2,1)} %x_in.1, bf16[2,128,1024]{2,1,0:T(8,128)(2,1)} %dy_in.1, ...), custom_call_target="tpu_custom_call" | custom-call | tf_op jit(solution)/shard_map/layer_backward/pallas_call | solution.py:584
  79.2 1.9 %store_outputs.1 = (bf16[2,128,1024]{2,1,0:T(8,128)(2,1)}, bf16[384,1024]{1,0:T(8,128)(2,1)}, bf16[128,1024]{1,0:T(8,128)(2,1)}, bf16[1024,512]{1,0:T(8,128)(2,1...) custom-call(bf16[2,128,1024]{2,1,0:T(8,128)(2,1)S(1)} %get-tuple-element.18.refs_0_, ...), custom_call_target="tpu_custom_call" | custom-call | tf_op jit(solution)/shard_map/store_outputs/pallas_call | solution.py:610

commit v5 on v4

--- a/solution.py
+++ b/solution.py
@@ -85,6 +85,9 @@
     def load(src, dst):
         loads.append(pltpu.make_async_copy(src, dst, load_sem.at[len(loads)]))
         loads[-1].start()
+
+    def load_piece(first, count, to):
+        pltpu.make_async_copy(wq_in.at[pl.ds(first, count), :], wq_ref.at[pl.ds(to, count), :], load_sem.at[2]).start()
 
     barrier = pltpu.get_barrier_semaphore()
     for target in (plus, minus, partner):
@@ -364,10 +367,10 @@
     for t, base in ((0, 0), (1, 2 * hd)):
         for part in range(2):
             for g in range(2):
-                load(wq_in.at[pl.ds(g * 3 * hd + t * hd + part * hh, hh), :],
-                     wq_ref.at[pl.ds(base + part * hd + g * hh, hh), :])
+                load_piece(g * 3 * hd + t * hd + part * hh, hh, base + part * hd + g * hh)
     for g in range(2):
-        load(wq_in.at[pl.ds(g * 3 * hd + 2 * hd, hd), :], wq_ref.at[pl.ds(4 * hd + g * hd, hd), :])
+        load_piece(g * 3 * hd + 2 * hd, hd, 4 * hd + g * hd)
+    loads.append(pltpu.make_async_copy(wq_in, wq_ref, load_sem.at[2]))
     load(cos_in, cos_ref)
     load(sin_in, sin_ref)
     load(wo_in, wo_ref)
@@ -400,35 +403,33 @@
                 send_ring(1)
                 service_second(0)
 
-            @pl.when(step == 1)
-            def _():
-                arrived(10, b)
-                arrived(11, b)
-
-            @pl.when(step == 2)
-            def _():
-                arrived(8, b)
-                arrived(9, b)
-
             @pl.when((step == 2) & (b == 1))
             def _():
                 add_partner(0, 1)
                 ring(6, 0).start()
                 add_partner(0, 2)
                 ring(8, 0).start()
-                add_partner(0, 3)
+
+            @pl.when(step == 1)
+            def _():
+                arrived(10, b)
+                arrived(11, b)
+
+            @pl.when(step == 2)
+            def _():
+                arrived(8, b)
+                arrived(9, b)
+
+            @pl.when(step == 3 - b)
+            def _():
+                service_far(b)
 
             @pl.when(step == 3)
             def _():
-                service_far(b)
                 arrived(12, b)
                 arrived(13, b)
 
             unit(jnp.where(step == 0, 1, b), lax.rem(chip + pick(jnp.maximum(step, 0), GATHER_ORDER), nc))
-
-        @pl.when(b == 0)
-        def _():
-            service_first(1)
 
         @pl.when(b == 1)
         def _():
@@ -441,9 +442,9 @@
         def _(h):
             attention_head(b, h)
 
-        @pl.when(b == 0)
-        def _():
-            service_second(1)
+            @pl.when((b == 0) & (h == 0))
+            def _():
+                service_first(1)
 
         @pl.loop(0, nc)
         def _(j):
@@ -452,6 +453,10 @@
                 @pl.when(j == jj)
                 def _(jj=jj):
                     to_partner(b, jj, SCATTER_ORDER[jj]).start()
+
+            @pl.when((b == 0) & (j == 1))
+            def _():
+                service_second(1)
 
             @pl.when(j == 3 - b)
             def _():
@@ -470,8 +475,6 @@
     gl_minus.start()
     ring(6, 1).start()
     ring(8, 1).start()
-    add_partner(1, 3)
-
     @pl.loop(0, width, step=BLK)
     def _(i):
         cols = pl.ds(pl.multiple_of(i, BLK), BLK)
@@ -512,6 +515,8 @@
             gq_ref[to:to + hd, cols] = total[row:row + hd]
         go_ref[:, cols] = out.astype(BF16)
 
+    add_partner(0, 3)
+    add_partner(1, 3)
     finish(0)
     gl_copy(2, from_chip(1), from_chip(1), minus).wait_recv()
     gl_copy(3, from_chip(2), from_chip(2), plus).wait_recv()
@@ -602,7 +607,7 @@
                 vm((seq, lanes), BF16), vm((seq, lanes), BF16), vm((seq, lanes), F32), vm((seq, lanes), F32),
                 vm((lanes, seq), F32), vm((batch, seq, 3 * lanes), BF16), vm((batch, lanes, seq), BF16),
                 vm((4, 8, width), F32), vm((nc, 4, width), F32), vm((2, 4, width), F32),
-                dma((17,)), dma((batch, 14)), dma((batch, 14)), dma((batch, 12)), dma((batch, 12)), dma((4,)), dma((4,)),
+                dma((8,)), dma((batch, 14)), dma((batch, 14)), dma((batch, 12)), dma((batch, 12)), dma((4,)), dma((4,)),
             ],
             compiler_params=pltpu.CompilerParams(collective_id=0, has_side_effects=True, vmem_limit_bytes=VMEM_LIMIT),
             name="layer_backward",

time: 81.3 us -> 79.4 us (0.977)
  Pallas kernels: 80.5 us -> 78.6 us
    pallas_call x1, Pallas kernels: 78.6 us -> 76.7 us  [device_step(): pl.pallas_call(functools.partial(layer_kernel, nt), out_shape=tuple((vm(s...]
where the time goes in v5:
time: 79.4 us; the launch traced here: 79.3 us
  Pallas kernels  78.6 us (99%)
    pallas_call x1, Pallas kernels, device_step(): pl.pallas_call(functools.partial(layer_kernel, nt), out_shape=tuple((vm(s...  76.7 us
    pallas_call x1, Pallas kernels, device_step(): pl.pallas_call(store_kernel, out_shape=shapes, in_specs=[vmem_spec] * 6,...  1.89 us

profile of v5, /device:TPU:81, one launch (start us, length us, event | category | flops | bytes accessed | tf_op | source)
XLA Modules:
  0.0 79.3 jit_solution(13958577330063126859)
XLA Ops:
  0.6 76.7 %layer_backward.1 = (bf16[2,128,1024]{2,1,0:T(8,128)(2,1)S(1)}, bf16[384,1024]{1,0:T(8,128)(2,1)S(1)}, bf16[128,1024]{1,0:T(8,128)(2,1)S(1)}, bf16[1024,512]{1,0...) custom-call(bf16[2,128,1024]{2,1,0:T(8,128)(2,1)} %x_in.1, bf16[2,128,1024]{2,1,0:T(8,128)(2,1)} %dy_in.1, ...), custom_call_target="tpu_custom_call" | custom-call | tf_op jit(solution)/shard_map/layer_backward/pallas_call | solution.py:589
  77.4 1.9 %store_outputs.1 = (bf16[2,128,1024]{2,1,0:T(8,128)(2,1)}, bf16[384,1024]{1,0:T(8,128)(2,1)}, bf16[128,1024]{1,0:T(8,128)(2,1)}, bf16[1024,512]{1,0:T(8,128)(2,1...) custom-call(bf16[2,128,1024]{2,1,0:T(8,128)(2,1)S(1)} %get-tuple-element.18.refs_0_, ...), custom_call_target="tpu_custom_call" | custom-call | tf_op jit(solution)/shard_map/store_outputs/pallas_call | solution.py:615

commit v6 on v5

--- a/solution.py
+++ b/solution.py
@@ -19,6 +19,8 @@
 MESH_ID = pl.DeviceIdType.MESH
 BLK = 256
 LN_ROWS = 32
+STORE_PARTS = 1
+KEY_BLK = 128
 VMEM_LIMIT = 62000000
 GATHER_ORDER = (0, 1, 3, 2)
 SCATTER_ORDER = (2, 1, 3, 0)
@@ -48,13 +50,13 @@
     return jnp.sum(value.reshape(rows // 8, 8, cols), axis=0)
 
 
-def layer_kernel(nt, x_in, dy_in, wq_in, wo_in, wu_in, wd_in, ln_ref, cos_in, sin_in,
+def layer_kernel(nt, x_in, dy_in, wq_in, wo_in, wu_in, wd_in, ln_in, cos_in, sin_in,
                  gi_ref, gq_ref, go_ref, gu_ref, gd_ref, gl_out,
                  x_ref, dy_ref, a_ref, m_ref, wq_ref, wo_ref, wu_ref, wd_ref, cos_ref, sin_ref,
                  q_ref, k_ref, v_ref, dc_ref, kt_ref, vt_ref, u_ref, dh_ref, t_ref, p_ref,
                  hp_ref, hm_ref, fp_ref, fm_ref, mu_ref, rstd_ref, s_ref, dp_ref, pt_ref, ds_ref,
                  qm_ref, dcm_ref, dka_ref, dva_ref, dqt_ref, dqkv_ref, ct_ref, acc_ref, gl_ref, gls_ref,
-                 load_sem, ag_send, ag_recv, rs_send, rs_recv, gl_send, gl_recv):
+                 ln_ref, load_sem, ag_send, ag_recv, rs_send, rs_recv, gl_send, gl_recv):
     nc = nt // 2
     batch, seq, width = x_ref.shape
     ff = wu_ref.shape[1]
@@ -89,19 +91,21 @@
     def load_piece(first, count, to):
         pltpu.make_async_copy(wq_in.at[pl.ds(first, count), :], wq_ref.at[pl.ds(to, count), :], load_sem.at[2]).start()
 
+    load(x_in, x_ref.at[:, pl.ds(row0(me), rows), :])
+    load(dy_in, dy_ref.at[:, pl.ds(row0(me), rows), :])
+
     barrier = pltpu.get_barrier_semaphore()
     for target in (plus, minus, partner):
         pl.semaphore_signal(barrier, inc=1, device_id={"tp": target}, device_id_type=MESH_ID)
 
-    load(x_in, x_ref.at[:, pl.ds(row0(me), rows), :])
-    load(dy_in, dy_ref.at[:, pl.ds(row0(me), rows), :])
     loads[0].wait()
     loads[1].wait()
     pl.semaphore_wait(barrier, 3)
 
     def ag(kind, src, dst, b, target):
+        send = ag_send.at[b * 6 + kind] if kind < 6 else ag_send.at[6 + kind]
         return pltpu.make_async_remote_copy(
-            src_ref=src, dst_ref=dst, send_sem=ag_send.at[b, kind], recv_sem=ag_recv.at[b, kind],
+            src_ref=src, dst_ref=dst, send_sem=send, recv_sem=ag_recv.at[b, kind],
             device_id={"tp": target}, device_id_type=MESH_ID)
 
     def rows_of(ref, b, device):
@@ -140,6 +144,9 @@
             own(kind, b).start()
 
     def service_first(b):
+        if b == 1:
+            for kind in range(6, 14):
+                forward(kind, 0).wait_send()
         arrived(0, b)
         forward(6, b).start()
         forward(8, b).start()
@@ -161,7 +168,7 @@
 
     def rs(kind, src, dst, b, target):
         return pltpu.make_async_remote_copy(
-            src_ref=src, dst_ref=dst, send_sem=rs_send.at[b, kind], recv_sem=rs_recv.at[b, kind],
+            src_ref=src, dst_ref=dst, send_sem=rs_send.at[kind], recv_sem=rs_recv.at[b, kind],
             device_id={"tp": target}, device_id_type=MESH_ID)
 
     def part_rows(b, device, first, count):
@@ -269,21 +276,21 @@
             qm = qm_ref[qs, :]
             dcm = dcm_ref[qs, :]
             top = None
-            for kb in range(qb + 1):
-                ks = slice(kb * BLK, (kb + 1) * BLK)
+            for kb in range(0, kl, KEY_BLK):
+                ks = slice(kb, kb + KEY_BLK)
                 s = dot_nt(k_ref[b, ks, :], qm)
-                if kb == qb:
-                    key = lax.broadcasted_iota(jnp.int32, (BLK, BLK), 0)
-                    query = lax.broadcasted_iota(jnp.int32, (BLK, BLK), 1)
-                    s = jnp.where(key <= query, s, NEG_BIG)
+                if kb >= qb * BLK:
+                    key = lax.broadcasted_iota(jnp.int32, (KEY_BLK, BLK), 0) + (kb - qb * BLK)
+                    query = lax.broadcasted_iota(jnp.int32, (KEY_BLK, BLK), 1)
+                    s = jnp.where(key <= query, s, NEG_BIG / scale)
                 s_ref[ks, :] = s
-                best = jnp.max(s.reshape(BLK // 8, 8, BLK), axis=0)
+                best = jnp.max(s.reshape(KEY_BLK // 8, 8, BLK), axis=0)
                 top = best if top is None else jnp.maximum(top, best)
             top = jnp.max(top, axis=0, keepdims=True)
             total = jnp.zeros((8, BLK), F32)
             weighted = jnp.zeros((8, BLK), F32)
-            for kb in range(qb + 1):
-                ks = slice(kb * BLK, (kb + 1) * BLK)
+            for kb in range(0, kl, KEY_BLK):
+                ks = slice(kb, kb + KEY_BLK)
                 e = jnp.exp2((s_ref[ks, :] - top) * (scale * LOG2E))
                 dpr = dot_nt(v_ref[b, ks, :], dcm)
                 s_ref[ks, :] = e
@@ -292,8 +299,8 @@
                 weighted += fold8(e * dpr)
             inv = 1.0 / jnp.sum(total, axis=0, keepdims=True)
             mean_dp = jnp.sum(weighted, axis=0, keepdims=True) * inv
-            for kb in range(qb + 1):
-                ks = slice(kb * BLK, (kb + 1) * BLK)
+            for kb in range(0, kl, KEY_BLK):
+                ks = slice(kb, kb + KEY_BLK)
                 p = s_ref[ks, :] * inv
                 pt_ref[ks, qs] = p.astype(BF16)
                 ds_ref[ks, qs] = (p * (dp_ref[ks, :] - mean_dp) * scale).astype(BF16)
@@ -371,6 +378,7 @@
     for g in range(2):
         load_piece(g * 3 * hd + 2 * hd, hd, 4 * hd + g * hd)
     loads.append(pltpu.make_async_copy(wq_in, wq_ref, load_sem.at[2]))
+    load(ln_in, ln_ref)
     load(cos_in, cos_ref)
     load(sin_in, sin_ref)
     load(wo_in, wo_ref)
@@ -437,6 +445,11 @@
 
         dka_ref[...] = jnp.zeros_like(dka_ref)
         dva_ref[...] = jnp.zeros_like(dva_ref)
+
+        @pl.when(b == 1)
+        def _():
+            for j in range(nc):
+                to_partner(0, j, SCATTER_ORDER[j]).wait_send()
 
         @pl.loop(0, 2)
         def _(h):
@@ -457,6 +470,11 @@
             @pl.when((b == 0) & (j == 1))
             def _():
                 service_second(1)
+
+            @pl.when((j == 2) & (b == 1))
+            def _():
+                for kind in (4, 5, 6, 8):
+                    ring(kind, 0).wait_send()
 
             @pl.when(j == 3 - b)
             def _():
@@ -494,6 +512,8 @@
 
     gl_copy(1, from_chip(nc - 1), from_chip(nc - 1), plus).wait_recv()
     gl_far.start()
+    for kind in (7, 9, 10, 11):
+        ring(kind, 0).wait_send()
     ring_second(1)
 
     @pl.loop(0, width, step=BLK)
@@ -528,12 +548,10 @@
     for b in range(batch):
         for kind in range(6):
             own(kind, b).wait_send()
-        for kind in range(6, 14):
-            forward(kind, b).wait_send()
-        for j in range(nc):
-            to_partner(b, j, SCATTER_ORDER[j]).wait_send()
-    for kind in range(4, 12):
-        ring(kind, 0).wait_send()
+    for kind in range(6, 14):
+        forward(kind, 1).wait_send()
+    for j in range(nc):
+        to_partner(1, j, SCATTER_ORDER[j]).wait_send()
     for kind in (4, 5, 6, 8):
         ring(kind, 1).wait_send()
     for copy in (gl_pair, gl_plus, gl_minus, gl_far):
@@ -545,7 +563,13 @@
 
 def store_kernel(*refs):
     n = len(refs) // 2
-    copies = [pltpu.make_async_copy(refs[i], refs[n + i], refs[2 * n].at[i]) for i in range(n)]
+    copies = []
+    for src, dst in zip(refs[:n], refs[n:2 * n]):
+        parts = STORE_PARTS if src.shape[-2] % (16 * STORE_PARTS) == 0 else 1
+        step = src.shape[-2] // parts
+        for i in range(parts):
+            at = (slice(None),) * (len(src.shape) - 2) + (pl.ds(i * step, step), slice(None))
+            copies.append(pltpu.make_async_copy(src.at[at], dst.at[at], refs[2 * n].at[len(copies)]))
     for copy in copies:
         copy.start()
     for copy in copies:
@@ -589,7 +613,7 @@
         outs = pl.pallas_call(
             functools.partial(layer_kernel, nt),
             out_shape=tuple(vm(shape.shape, shape.dtype) for shape in shapes),
-            in_specs=[any_spec] * 6 + [vmem_spec] + [any_spec] * 2,
+            in_specs=[any_spec] * 9,
             out_specs=(vmem_spec,) * 6,
             scratch_shapes=[
                 vm((batch, seq, width), BF16), vm((batch, seq, width), BF16),
@@ -607,7 +631,7 @@
                 vm((seq, lanes), BF16), vm((seq, lanes), BF16), vm((seq, lanes), F32), vm((seq, lanes), F32),
                 vm((lanes, seq), F32), vm((batch, seq, 3 * lanes), BF16), vm((batch, lanes, seq), BF16),
                 vm((4, 8, width), F32), vm((nc, 4, width), F32), vm((2, 4, width), F32),
-                dma((8,)), dma((batch, 14)), dma((batch, 14)), dma((batch, 12)), dma((batch, 12)), dma((4,)), dma((4,)),
+                vm((4, width), F32), dma((9,)), dma((20,)), dma((batch, 14)), dma((12,)), dma((batch, 12)), dma((4,)), dma((4,)),
             ],
             compiler_params=pltpu.CompilerParams(collective_id=0, has_side_effects=True, vmem_limit_bytes=VMEM_LIMIT),
             name="layer_backward",
@@ -617,7 +641,7 @@
             out_shape=shapes,
             in_specs=[vmem_spec] * 6,
             out_specs=(any_spec,) * 6,
-            scratch_shapes=[dma((6,))],
+            scratch_shapes=[dma((6 * STORE_PARTS,))],
             compiler_params=pltpu.CompilerParams(vmem_limit_bytes=1 << 20),
             name="store_outputs",
         )(*(pltpu.with_memory_space_constraint(out, pltpu.VMEM) for out in outs))

time: 79.4 us -> 78.3 us (0.986)
  Pallas kernels: 78.6 us -> 77.6 us
    pallas_call x1, Pallas kernels: 76.7 us -> 75.7 us  [device_step(): pl.pallas_call(functools.partial(layer_kernel, nt), out_shape=tuple((vm(s...]
where the time goes in v6:
time: 78.3 us; the launch traced here: 78.2 us
  Pallas kernels  77.6 us (99%)
    pallas_call x1, Pallas kernels, device_step(): pl.pallas_call(functools.partial(layer_kernel, nt), out_shape=tuple((vm(s...  75.7 us
    pallas_call x1, Pallas kernels, device_step(): pl.pallas_call(store_kernel, out_shape=shapes, in_specs=[vmem_spec] * 6,...  1.89 us

profile of v6, /device:TPU:81, one launch (start us, length us, event | category | flops | bytes accessed | tf_op | source)
XLA Modules:
  0.0 78.2 jit_solution(3760017486442299911)
XLA Ops:
  0.6 75.7 %layer_backward.1 = (bf16[2,128,1024]{2,1,0:T(8,128)(2,1)S(1)}, bf16[384,1024]{1,0:T(8,128)(2,1)S(1)}, bf16[128,1024]{1,0:T(8,128)(2,1)S(1)}, bf16[1024,512]{1,0...) custom-call(bf16[2,128,1024]{2,1,0:T(8,128)(2,1)} %x_in.1, bf16[2,128,1024]{2,1,0:T(8,128)(2,1)} %dy_in.1, ...), custom_call_target="tpu_custom_call" | custom-call | tf_op jit(solution)/shard_map/layer_backward/pallas_call | solution.py:613
  76.3 1.9 %store_outputs.1 = (bf16[2,128,1024]{2,1,0:T(8,128)(2,1)}, bf16[384,1024]{1,0:T(8,128)(2,1)}, bf16[128,1024]{1,0:T(8,128)(2,1)}, bf16[1024,512]{1,0:T(8,128)(2,1...) custom-call(bf16[2,128,1024]{2,1,0:T(8,128)(2,1)S(1)} %get-tuple-element.18.refs_0_, ...), custom_call_target="tpu_custom_call" | custom-call | tf_op jit(solution)/shard_map/store_outputs/pallas_call | solution.py:639

commit v7 on v6

--- a/solution.py
+++ b/solution.py
@@ -242,6 +242,10 @@
         v_ref[b, at, :] = v.astype(BF16)
         vt_ref[b, :, at] = v.T.astype(BF16)
         dc_ref[b, at, :] = dot_nt(dy, wo_ref[...]).astype(BF16)
+
+    def unit_mlp(b, cc):
+        at = pl.ds(pl.multiple_of(cc * pair, pair), pair)
+        dy = dy_ref[b, at, :]
         m = m_ref[b, at, :]
         for f in range(0, ff, BLK):
             h = dot_nn(m, wu_ref[:, f:f + BLK])
@@ -437,7 +441,12 @@
                 arrived(12, b)
                 arrived(13, b)
 
-            unit(jnp.where(step == 0, 1, b), lax.rem(chip + pick(jnp.maximum(step, 0), GATHER_ORDER), nc))
+            which, cc = jnp.where(step == 0, 1, b), lax.rem(chip + pick(jnp.maximum(step, 0), GATHER_ORDER), nc)
+            unit(which, cc)
+
+            @pl.when((b == 0) | (step == 3))
+            def _():
+                unit_mlp(which, cc)
 
         @pl.when(b == 1)
         def _():
@@ -461,6 +470,10 @@
 
         @pl.loop(0, nc)
         def _(j):
+            @pl.when((b == 1) & (j > 0) & (j < 3))
+            def _():
+                unit_mlp(1, lax.rem(chip + pick(j, SCATTER_ORDER), nc))
+
             input_grad(b, lax.rem(chip + pick(j, SCATTER_ORDER), nc))
             for jj in range(nc):
                 @pl.when(j == jj)
@@ -471,12 +484,12 @@
             def _():
                 service_second(1)
 
-            @pl.when((j == 2) & (b == 1))
+            @pl.when((j == 1) & (b == 1))
             def _():
                 for kind in (4, 5, 6, 8):
                     ring(kind, 0).wait_send()
 
-            @pl.when(j == 3 - b)
+            @pl.when(j == 3 - 2 * b)
             def _():
                 add_partner(b, 0)
                 ring(4, b).start()

time: 78.3 us -> 78.1 us (level)
  no operation moved by 1% of the time
where the time goes in v7:
time: 78.1 us; the launch traced here: 78 us
  Pallas kernels  77.3 us (99%)
    pallas_call x1, Pallas kernels, device_step(): pl.pallas_call(functools.partial(layer_kernel, nt), out_shape=tuple((vm(s...  75.4 us
    pallas_call x1, Pallas kernels, device_step(): pl.pallas_call(store_kernel, out_shape=shapes, in_specs=[vmem_spec] * 6,...  1.89 us

profile of v7, /device:TPU:81, one launch (start us, length us, event | category | flops | bytes accessed | tf_op | source)
XLA Modules:
  0.0 78.0 jit_solution(11702230244997272621)
XLA Ops:
  0.6 75.4 %layer_backward.1 = (bf16[2,128,1024]{2,1,0:T(8,128)(2,1)S(1)}, bf16[384,1024]{1,0:T(8,128)(2,1)S(1)}, bf16[128,1024]{1,0:T(8,128)(2,1)S(1)}, bf16[1024,512]{1,0...) custom-call(bf16[2,128,1024]{2,1,0:T(8,128)(2,1)} %x_in.1, bf16[2,128,1024]{2,1,0:T(8,128)(2,1)} %dy_in.1, ...), custom_call_target="tpu_custom_call" | custom-call | tf_op jit(solution)/shard_map/layer_backward/pallas_call | solution.py:626
  76.1 1.9 %store_outputs.1 = (bf16[2,128,1024]{2,1,0:T(8,128)(2,1)}, bf16[384,1024]{1,0:T(8,128)(2,1)}, bf16[128,1024]{1,0:T(8,128)(2,1)}, bf16[1024,512]{1,0:T(8,128)(2,1...) custom-call(bf16[2,128,1024]{2,1,0:T(8,128)(2,1)S(1)} %get-tuple-element.18.refs_0_, ...), custom_call_target="tpu_custom_call" | custom-call | tf_op jit(solution)/shard_map/store_outputs/pallas_call | solution.py:652
